TPU v7x, 32 devices: a whole 2x2x4 slice. The times are simulated.
32 devices in a mesh: gx: 4 (over x, core), gy: 4 (over z), gz: 2 (over y).
Axes of the slice: x: 2, y: 2, z: 4, core: 2. Of those that a mesh axis runs over, the one named last changes fastest.
Arguments:
- right_side: float32 [16, 16, 8, 4, 256], P('gx', 'gy', 'gz'), may hold values from -80 to 80
- bond_blocks: float32 [13, 4, 4, 16, 16, 8], P(None, None, None, 'gx', 'gy', 'gz'), may hold values from -0.012 to 0.012
- bond_open: int32 [13, 16, 16, 8], P(None, 'gx', 'gy', 'gz'), may hold values 0 or 1
- onsite_blocks: float32 [4, 4, 16, 16, 8], P(None, None, 'gx', 'gy', 'gz'), may hold values from -0.012 to 0.012
- orbital_levels: float32 [4, 16, 16, 8], P(None, 'gx', 'gy', 'gz'), may hold values from 1.3 to 2.6
- column_shift: float32 [256], replicated, may hold values from 0.05 to 1
Outputs:
- solution: float32 [16, 16, 8, 4, 256], P('gx', 'gy', 'gz')
- residual: float32 [16, 16, 8, 4, 256], P('gx', 'gy', 'gz')
All inputs are finite; a program needn't handle non-finite values. No bound on the sum of `bond_open` on one device may be relied on, other than what follows from the above.
Results may differ from a plain program's by a relative error of at most 0.0003.
Values sent between devices are 32-bit elements; how exact they have to be, the bound alone decides.
No kernel may reach another device: no remote copies, remote signals or barrier semaphores. Data moves between devices by JAX's collectives and lax.ppermute only.
A program may use at most 192 MiB of HBM per device.

v0:
```python
import jax
import jax.numpy as jnp
from jax import lax
from jax.sharding import PartitionSpec as P

ITERS = 3


half_offsets = [
    (first, second, third)
    for first in (-1, 0, 1)
    for second in (-1, 0, 1)
    for third in (-1, 0, 1)
    if (first, second, third) > (0, 0, 0)
]


def extended_2(cells, sides, width):
    for axis, dim in sides:
        count = lax.axis_size(axis)
        head = lax.slice_in_dim(cells, 0, width, axis=dim)
        tail = lax.slice_in_dim(cells, cells.shape[dim] - width, cells.shape[dim], axis=dim)
        cells = jnp.concatenate(
            [
                lax.ppermute(tail, axis, [(i, (i + 1) % count) for i in range(count)]),
                cells,
                lax.ppermute(head, axis, [((i + 1) % count, i) for i in range(count)]),
            ],
            axis=dim,
        )
    return cells


def shifted(value, axis, by):
    peers = lax.axis_size(axis)
    return lax.ppermute(value, axis, [(i, (i + by) % peers) for i in range(peers)])


def block_apply(blocks, vector, flipped):
    orbitals = vector.shape[3]
    rows = []
    for out_orb in range(orbitals):
        total = None
        for in_orb in range(orbitals):
            factor = blocks[in_orb, out_orb] if flipped else blocks[out_orb, in_orb]
            term = factor[..., None] * vector[:, :, :, in_orb, :]
            total = term if total is None else total + term
        rows.append(total)
    return jnp.stack(rows, axis=3)


def hop(blocks, vector):
    return block_apply(blocks, vector, False)


def hop_back(blocks, vector):
    return block_apply(blocks, vector, True)


def window(extended, offset, counts, base_first):
    return extended[
        base_first + offset[0] : base_first + offset[0] + counts[0],
        1 + offset[1] : 1 + offset[1] + counts[1],
        1 + offset[2] : 1 + offset[2] + counts[2],
    ]


def outer_layer(extended, dim, upper):
    inner = extended.shape[dim] - 2
    if upper:
        return lax.slice_in_dim(extended, inner + 1, inner + 2, axis=dim)
    return lax.slice_in_dim(extended, 0, 1, axis=dim)


def settle(extended, dim, from_lower, from_upper):
    inner = extended.shape[dim] - 2
    core = lax.slice_in_dim(extended, 1, inner + 1, axis=dim)
    pads_lower = [(0, 0)] * extended.ndim
    pads_upper = [(0, 0)] * extended.ndim
    pads_lower[dim] = (0, inner - 1)
    pads_upper[dim] = (inner - 1, 0)
    return core + jnp.pad(from_lower, pads_lower) + jnp.pad(from_upper, pads_upper)


def settle_first(extended, from_lower):
    inner = extended.shape[0] - 1
    core = extended[:inner]
    pads_lower = [(0, 0)] * extended.ndim
    pads_lower[0] = (0, inner - 1)
    return core + jnp.pad(from_lower, pads_lower)


def per_device(right_side, bond_blocks, bond_open, onsite_blocks, orbital_levels, column_shift):
    coupled = bond_blocks * bond_open[:, None, None].astype(jnp.float32)
    onsite_sym = 0.5 * (onsite_blocks + jnp.swapaxes(onsite_blocks, 0, 1))
    atom_levels = jnp.transpose(orbital_levels, (1, 2, 3, 0))
    counts = right_side.shape[:3]

    def operate(vector):
        result = hop(onsite_sym, vector) + (atom_levels[..., None] + column_shift) * vector
        side = extended_2(vector, (("gy", 1), ("gz", 2)), 1)
        following = shifted(side[0:1], "gx", -1)
        extended = jnp.concatenate([side, following], axis=0)
        for bond_index, offset in enumerate(half_offsets):
            result = result + hop(coupled[bond_index], window(extended, offset, counts, 0))
        spilled = jnp.zeros(
            (counts[0] + 1, counts[1] + 2, counts[2] + 2) + vector.shape[3:], jnp.float32
        )
        for bond_index, offset in enumerate(half_offsets):
            placed = (
                (offset[0], 1 - offset[0]),
                (1 + offset[1], 1 - offset[1]),
                (1 + offset[2], 1 - offset[2]),
                (0, 0),
                (0, 0),
            )
            spilled = spilled + jnp.pad(hop_back(coupled[bond_index], vector), placed)
        top_layer = spilled[counts[0] : counts[0] + 1]
        spilled = settle_first(spilled, shifted(top_layer, "gx", 1))
        spilled = settle(
            spilled,
            1,
            shifted(outer_layer(spilled, 1, True), "gy", 1),
            shifted(outer_layer(spilled, 1, False), "gy", -1),
        )
        spilled = settle(
            spilled,
            2,
            shifted(outer_layer(spilled, 2, True), "gz", 1),
            shifted(outer_layer(spilled, 2, False), "gz", -1),
        )
        result = result + spilled
        return result

    def two_products(residual, image):
        return lax.psum(
            (
                jnp.sum(residual * residual, axis=(0, 1, 2, 3)),
                jnp.sum(residual * image, axis=(0, 1, 2, 3)),
            ),
            ("gx", "gy", "gz"),
        )

    solution = jnp.zeros_like(right_side)
    residual = right_side
    image = operate(residual)
    norm_now, product = two_products(residual, image)
    alpha = norm_now / product
    direction = residual
    along = image
    for iteration in range(ITERS):
        solution = solution + alpha * direction
        residual = residual - alpha * along
        if iteration + 1 < ITERS:
            image = operate(residual)
            norm_next, product = two_products(residual, image)
            ratio = norm_next / norm_now
            alpha = norm_next / (product - ratio * norm_next / alpha)
            direction = residual + ratio * direction
            along = image + ratio * along
            norm_now = norm_next
    return (solution, residual)


def solution(mesh):
    placed = (
        P("gx", "gy", "gz", None, None),
        P(None, None, None, "gx", "gy", "gz"),
        P(None, "gx", "gy", "gz"),
        P(None, None, "gx", "gy", "gz"),
        P(None, "gx", "gy", "gz"),
        P(),
    )
    return jax.shard_map(
        per_device,
        mesh=mesh,
        in_specs=placed,
        out_specs=(P("gx", "gy", "gz", None, None), P("gx", "gy", "gz", None, None)),
        check_vma=False,
    )
```

profile of v0, /device:TPU:0, one launch (start us, length us, event | category | flops | bytes accessed | tf_op | source)
XLA Modules:
  0.0 348.6 jit_solution(13338031472730461448)
XLA Ops:
  0.6 1.5 fusion.136
  2.2 3.1 collective-permute-start
  5.2 1.1 broadcast_multiply_fusion
  6.3 8.4 %slice_reduce_fusion.12 = (f32[4,4,4,4,4]{4,3,2,1,0:T(4,128)S(1)}, f32[4,4,4,4,4]{4,3,2,1,0:T(4,128)S(1)}, f32[4,4,4,4,4]{4,3,2,1,0:T(4,128)S(1)}, f32[4,4,4,4,4...) fusion(f32[13,4,4,4,4,4]{0,5,4,3,2,1:T(4,128)S(1)} %bitcast.456), kind=kLoop, calls=%fused_computation.212 | loop fusion | bytes 106496 | tf_op jit(solution)/shard_map/slice | solution.py:105
  15.1 0.9 copy-done.33
  16.2 0.8 copy-done
  16.9 1.2 multiply_add_fusion.219
  18.8 0.7 multiply_add_fusion.223
  20.2 0.7 multiply_add_fusion.227
  21.0 0.7 multiply_add_fusion.229
  21.7 0.7 multiply_add_fusion.231
  23.2 0.7 multiply_add_fusion.235
  23.9 0.7 multiply_add_fusion.237
  24.6 0.7 multiply_add_fusion.239
  29.7 0.7 multiply_add_fusion.253
  30.4 0.7 multiply_add_fusion.255
  31.2 0.7 multiply_add_fusion.257
  37.8 8.6 %fusion.36 = f32[5,6,6,4,256]{4,3,2,1,0:T(4,128)S(1)} fusion(f32[4,4,4,1,256]{4,3,2,1,0:T(1,128)S(1)} %get-tuple-element.412, f32[4,4,4,1,256]{4,3,2,1,0:T(1,128)S(1)} %get-tuple-element.411, f32[4,4,4,1,256]{4,3,2,1,0:T(1,128)S(1)} %get-tuple-element.410, f32[4,4,4,1,256]{4,3,2,1,0:T(1,128)S(1)} %get-tuple-element.409, ...), kind=kLoop, calls=%fused_computation.126 | loop fusion | flops 44421120 | bytes 4145152 | tf_op jit(solution)/shard_map/add | solution.py:117
  46.6 2.1 collective-permute-start.1
  48.9 0.8 constant_dynamic-update-slice_fusion.2
  49.8 1.4 collective-permute-done.1
  51.3 1.6 collective-permute-start.2
  55.0 3.7 %collective-permute-start.7 = (f32[4,1,6,4,256]{4,3,2,1,0:T(4,128)S(1)}, f32[4,1,6,4,256]{4,3,2,1,0:T(4,128)S(1)}, u32[]{:S(2)}, u32[]{:S(2)}) collective-permute-start(f32[4,1,6,4,256]{4,3,2,1,0:T(4,128)S(1)} %get-tuple-element.183), channel_id=1, source_target_pairs={{0,6},{2,0},{4,2},{6,4},{1,7},{3,1},{5,3},{7,5},{8,14},{10,8},{12,... | collective-permute-start | bytes 294920 | tf_op jit(solution)/shard_map/ppermute | solution.py:36
  59.9 1.0 multiply_add_fusion.308
  61.4 1.0 multiply_add_fusion.316
  63.0 1.0 multiply_add_fusion.320
  64.0 1.2 collective-permute-done.6
  65.2 1.9 collective-permute-start.9
  81.3 4.0 %multiply_reduce_fusion.4 = (f32[256]{0:T(256)S(1)}, f32[256]{0:T(256)S(1)}, f32[4,4,4,4,256]{4,3,2,1,0:T(4,128)S(1)}) fusion(f32[4,4,4,4,256]{4,3,2,1,0:T(4,128)S(1)} %copy-done, f32[4,4,1,4,256]{4,3,2,1,0:T(4,128)S(1)} %collective-permute-done.9, f32[4,4,1,4,256]{4,3,2,1,0:T(4,128)S(1)} %collective-permute-done.8, f32[4,4,6,4,256]{4,3,2,1,0:T(4,128)S(1)} %fusion.62, ...), kind=kLoop, calls=%fused_computation.291 | loop fusion | flops 4259328 | bytes 4591616 | tf_op jit(solution)/shard_map/reduce_sum | solution.py:139
  85.2 39.4 %all-reduce.56 = (f32[256]{0:T(256)S(1)}, f32[256]{0:T(256)S(1)}) all-reduce(f32[256]{0:T(256)S(1)} %get-tuple-element.20, f32[256]{0:T(256)S(1)} %get-tuple-element.19), channel_id=1, replica_groups=mesh['gx'=4,'gy'=4,'gz'=2] {'gx','gy','gz'}, use_global_device_ids=true, to_apply=%region_1.2 | all-reduce | flops 512 | bytes 4096 | tf_op jit(solution)/shard_map/psum | solution.py:136
  139.2 0.7 multiply_add_fusion.159
  144.6 1.6 collective-permute-start.11
  147.2 1.8 collective-permute-done.11
  149.0 0.7 multiply_add_fusion.205
  149.8 8.6 %fusion.24 = f32[5,6,6,4,256]{4,3,2,1,0:T(4,128)S(1)} fusion(f32[4,4,4,1,256]{4,3,2,1,0:T(1,128)S(1)} %multiply_add_fusion.110, f32[4,4,4,1,256]{4,3,2,1,0:T(1,128)S(1)} %get-tuple-element.343, f32[4,4,4,1,256]{4,3,2,1,0:T(1,128)S(1)} %get-tuple-element.342, f32[4,4,4,1,256]{4,3,2,1,0:T(1,128)S(1)} %get-tuple-element.341, ...), kind=kLoop, calls=%fused_computation.75 | loop fusion | flops 44421120 | bytes 4145152 | tf_op jit(solution)/shard_map/add | solution.py:117
  159.0 2.3 collective-permute-start.12
  161.4 1.0 multiply_add_fusion.204
  162.4 2.1 collective-permute-done.12
  167.0 0.9 collective-permute-start.14
  168.4 1.0 multiply_add_fusion.208
  170.3 3.3 collective-permute-start.17
  186.2 2.4 collective-permute-start.19
  189.4 2.1 collective-permute-done.19
  191.5 1.4 collective-permute-done.18
  192.9 4.0 %multiply_reduce_fusion.2 = (f32[256]{0:T(256)S(1)}, f32[256]{0:T(256)S(1)}, f32[4,4,4,4,256]{4,3,2,1,0:T(4,128)S(1)}) fusion(f32[4,4,4,4,256]{4,3,2,1,0:T(4,128)S(1)} %multiply_subtract_fusion.2, f32[4,4,1,4,256]{4,3,2,1,0:T(4,128)S(1)} %collective-permute-done.19, f32[4,4,1,4,256]{4,3,2,1,0:T(4,128)S(1)} %collective-permute-done.18, ...), kind=kLoop, calls=%fused_computation.288 | loop fusion | flops 4259328 | bytes 4591616 | tf_op jit(solution)/shard_map/reduce_sum | solution.py:139
  196.9 39.3 %all-reduce.55 = (f32[256]{0:T(256)S(1)}, f32[256]{0:T(256)S(1)}) all-reduce(f32[256]{0:T(256)S(1)} %get-tuple-element.18, f32[256]{0:T(256)S(1)} %get-tuple-element.17), channel_id=1, replica_groups=mesh['gx'=4,'gy'=4,'gz'=2] {'gx','gy','gz'}, use_global_device_ids=true, to_apply=%region_5.6 | all-reduce | flops 512 | bytes 4096 | tf_op jit(solution)/shard_map/psum | solution.py:136
  236.3 0.7 multiply_add_fusion.4
  252.3 0.7 multiply_add_fusion.53
  255.9 1.6 collective-permute-start.21
  258.6 1.8 collective-permute-done.21
  260.4 0.7 multiply_add_fusion.97
  261.2 8.6 %fusion.12 = f32[5,6,6,4,256]{4,3,2,1,0:T(4,128)S(1)} fusion(f32[4,4,4,1,256]{4,3,2,1,0:T(1,128)S(1)} %multiply_add_fusion.2, f32[4,4,4,1,256]{4,3,2,1,0:T(1,128)S(1)} %get-tuple-element.281, f32[4,4,4,1,256]{4,3,2,1,0:T(1,128)S(1)} %get-tuple-element.280, f32[4,4,4,1,256]{4,3,2,1,0:T(1,128)S(1)} %get-tuple-element.279, ...), kind=kLoop, calls=%fused_computation.24 | loop fusion | flops 44421120 | bytes 4145152 | tf_op jit(solution)/shard_map/add | solution.py:117
  270.2 2.3 collective-permute-start.22
  272.6 1.0 multiply_add_fusion.96
  273.6 2.1 collective-permute-done.22
  278.2 0.9 collective-permute-start.24
  279.6 1.0 multiply_add_fusion.100
  281.5 3.2 collective-permute-start.27
  297.4 2.4 collective-permute-start.29
  300.6 2.1 collective-permute-done.29
  302.7 1.4 collective-permute-done.28
  304.0 4.0 %multiply_reduce_fusion = (f32[256]{0:T(256)S(1)}, f32[256]{0:T(256)S(1)}, f32[4,4,4,4,256]{4,3,2,1,0:T(4,128)S(1)}) fusion(f32[4,4,4,4,256]{4,3,2,1,0:T(4,128)S(1)} %multiply_subtract_fusion.1, f32[4,4,1,4,256]{4,3,2,1,0:T(4,128)S(1)} %collective-permute-done.29, f32[4,4,1,4,256]{4,3,2,1,0:T(4,128)S(1)} %collective-permute-done.28, ...), kind=kLoop, calls=%fused_computation.284 | loop fusion | flops 4259328 | bytes 4591616 | tf_op jit(solution)/shard_map/reduce_sum | solution.py:139
  308.0 39.1 %all-reduce.54 = (f32[256]{0:T(256)S(1)}, f32[256]{0:T(256)S(1)}) all-reduce(f32[256]{0:T(256)S(1)} %get-tuple-element.16, f32[256]{0:T(256)S(1)} %get-tuple-element.15), channel_id=1, replica_groups=mesh['gx'=4,'gy'=4,'gz'=2] {'gx','gy','gz'}, use_global_device_ids=true, to_apply=%region_9.10 | all-reduce | flops 512 | bytes 4096 | tf_op jit(solution)/shard_map/psum | solution.py:136
  347.2 1.2 multiply_subtract_fusion
  (298 shorter events, 105.4 us)
Async XLA Ops:
  0.6 4.6 %copy-start.34 = (s32[13,4,4,4]{0,3,2,1:T(4,128)S(1)}, s32[13,4,4,4]{0,3,2,1:T(4,128)}, u32[]{:S(2)}) copy-start(s32[13,4,4,4]{0,3,2,1:T(4,128)} %param.8) | copy-start | bytes 9988
  2.2 46.7 %collective-permute-start = (f32[4,1,4,4,256]{4,3,2,1,0:T(4,128)}, f32[4,1,4,4,256]{4,3,2,1,0:T(4,128)}, u32[]{:S(2)}, u32[]{:S(2)}) collective-permute-start(f32[4,1,4,4,256]{4,3,2,1,0:T(4,128)} %get-tuple-element.364), channel_id=1, source_target_pairs={{0,2},{2,4},{4,6},{6,0},{1,3},{3,5},{5,7},{7,1},{8,10},{10,12},{12... | collective-permute-start | bytes 196616 | tf_op jit(solution)/shard_map/ppermute | solution.py:25
  15.0 0.9 copy-start.33
  15.9 1.0 copy-start
  16.0 18.8 %copy-start.25 = (f32[4,4,4]{2,1,0:T(4,128)}, f32[4,4,4]{2,1,0:T(4,128)S(1)}, u32[]{:S(2)}) copy-start(f32[4,4,4]{2,1,0:T(4,128)S(1)} %get-tuple-element.414) | copy-start | bytes 772
  16.0 18.8 %copy-start.27 = (f32[4,4,4]{2,1,0:T(4,128)}, f32[4,4,4]{2,1,0:T(4,128)S(1)}, u32[]{:S(2)}) copy-start(f32[4,4,4]{2,1,0:T(4,128)S(1)} %get-tuple-element.415) | copy-start | bytes 772
  16.0 18.8 %copy-start.29 = (f32[4,4,4]{2,1,0:T(4,128)}, f32[4,4,4]{2,1,0:T(4,128)S(1)}, u32[]{:S(2)}) copy-start(f32[4,4,4]{2,1,0:T(4,128)S(1)} %get-tuple-element.416) | copy-start | bytes 772
  16.0 18.8 %copy-start.31 = (f32[4,4,4]{2,1,0:T(4,128)}, f32[4,4,4]{2,1,0:T(4,128)S(1)}, u32[]{:S(2)}) copy-start(f32[4,4,4]{2,1,0:T(4,128)S(1)} %get-tuple-element.417) | copy-start | bytes 772
  16.0 19.5 %copy-start.17 = (f32[4,4,4]{2,1,0:T(4,128)}, f32[4,4,4]{2,1,0:T(4,128)S(1)}, u32[]{:S(2)}) copy-start(f32[4,4,4]{2,1,0:T(4,128)S(1)} %get-tuple-element.418) | copy-start | bytes 772
  16.0 19.5 %copy-start.19 = (f32[4,4,4]{2,1,0:T(4,128)}, f32[4,4,4]{2,1,0:T(4,128)S(1)}, u32[]{:S(2)}) copy-start(f32[4,4,4]{2,1,0:T(4,128)S(1)} %get-tuple-element.419) | copy-start | bytes 772
  16.1 19.5 %copy-start.21 = (f32[4,4,4]{2,1,0:T(4,128)}, f32[4,4,4]{2,1,0:T(4,128)S(1)}, u32[]{:S(2)}) copy-start(f32[4,4,4]{2,1,0:T(4,128)S(1)} %get-tuple-element.420) | copy-start | bytes 772
  16.1 19.5 %copy-start.23 = (f32[4,4,4]{2,1,0:T(4,128)}, f32[4,4,4]{2,1,0:T(4,128)S(1)}, u32[]{:S(2)}) copy-start(f32[4,4,4]{2,1,0:T(4,128)S(1)} %get-tuple-element.421) | copy-start | bytes 772
  16.1 20.2 %copy-start.9 = (f32[4,4,4]{2,1,0:T(4,128)}, f32[4,4,4]{2,1,0:T(4,128)S(1)}, u32[]{:S(2)}) copy-start(f32[4,4,4]{2,1,0:T(4,128)S(1)} %get-tuple-element.422) | copy-start | bytes 772
  16.1 20.2 %copy-start.11 = (f32[4,4,4]{2,1,0:T(4,128)}, f32[4,4,4]{2,1,0:T(4,128)S(1)}, u32[]{:S(2)}) copy-start(f32[4,4,4]{2,1,0:T(4,128)S(1)} %get-tuple-element.423) | copy-start | bytes 772
  16.1 20.2 %copy-start.13 = (f32[4,4,4]{2,1,0:T(4,128)}, f32[4,4,4]{2,1,0:T(4,128)S(1)}, u32[]{:S(2)}) copy-start(f32[4,4,4]{2,1,0:T(4,128)S(1)} %get-tuple-element.424) | copy-start | bytes 772
  16.1 20.2 %copy-start.15 = (f32[4,4,4]{2,1,0:T(4,128)}, f32[4,4,4]{2,1,0:T(4,128)S(1)}, u32[]{:S(2)}) copy-start(f32[4,4,4]{2,1,0:T(4,128)S(1)} %get-tuple-element.425) | copy-start | bytes 772
  16.1 21.0 %copy-start.1 = (f32[4,4,4]{2,1,0:T(4,128)}, f32[4,4,4]{2,1,0:T(4,128)S(1)}, u32[]{:S(2)}) copy-start(f32[4,4,4]{2,1,0:T(4,128)S(1)} %get-tuple-element.413) | copy-start | bytes 772
  16.1 21.0 %copy-start.3 = (f32[4,4,4]{2,1,0:T(4,128)}, f32[4,4,4]{2,1,0:T(4,128)S(1)}, u32[]{:S(2)}) copy-start(f32[4,4,4]{2,1,0:T(4,128)S(1)} %get-tuple-element.426) | copy-start | bytes 772
  16.1 21.0 %copy-start.5 = (f32[4,4,4]{2,1,0:T(4,128)}, f32[4,4,4]{2,1,0:T(4,128)S(1)}, u32[]{:S(2)}) copy-start(f32[4,4,4]{2,1,0:T(4,128)S(1)} %get-tuple-element.427) | copy-start | bytes 772
  16.1 21.0 %copy-start.7 = (f32[4,4,4]{2,1,0:T(4,128)}, f32[4,4,4]{2,1,0:T(4,128)S(1)}, u32[]{:S(2)}) copy-start(f32[4,4,4]{2,1,0:T(4,128)S(1)} %get-tuple-element.428) | copy-start | bytes 772
  46.5 2.2 copy-start.35
  46.5 8.3 %collective-permute-start.5 = (f32[1,6,6,4,256]{4,3,2,1,0:T(4,128)S(1)}, f32[1,6,6,4,256]{4,3,2,1,0:T(4,128)S(1)}, u32[]{:S(2)}, u32[]{:S(2)}) collective-permute-start(f32[1,6,6,4,256]{4,3,2,1,0:T(4,128)S(1)} %slice.1794), channel_id=1, source_target_pairs={{0,8},{8,16},{16,24},{24,0},{1,9},{9,17},{17,25},{25,1},{2,10},{10... | collective-permute-start | bytes 442376 | tf_op jit(solution)/shard_map/ppermute | solution.py:36
  46.6 4.7 %collective-permute-start.1 = (f32[4,1,4,4,256]{4,3,2,1,0:T(4,128)}, f32[4,1,4,4,256]{4,3,2,1,0:T(4,128)S(1)}, u32[]{:S(2)}, u32[]{:S(2)}) collective-permute-start(f32[4,1,4,4,256]{4,3,2,1,0:T(4,128)} %get-tuple-element.363), channel_id=1, source_target_pairs={{2,0},{4,2},{6,4},{0,6},{3,1},{5,3},{7,5},{1,7},{10,8},{12,10},{14... | collective-permute-start | bytes 196616 | tf_op jit(solution)/shard_map/ppermute | solution.py:27
  51.3 7.4 %collective-permute-start.2 = (f32[4,6,1,4,256]{4,3,2,1,0:T(4,128)S(1)}, f32[4,6,1,4,256]{4,3,2,1,0:T(4,128)S(1)}, u32[]{:S(2)}, u32[]{:S(2)}) collective-permute-start(f32[4,6,1,4,256]{4,3,2,1,0:T(4,128)S(1)} %get-tuple-element.209), channel_id=1, source_target_pairs={{1,0},{0,1},{3,2},{2,3},{5,4},{4,5},{7,6},{6,7},{9,8},{8,9},{11,10... | collective-permute-start | bytes 294920 | tf_op jit(solution)/shard_map/ppermute | solution.py:27
  52.9 5.9 %collective-permute-start.3 = (f32[4,6,1,4,256]{4,3,2,1,0:T(4,128)S(1)}, f32[4,6,1,4,256]{4,3,2,1,0:T(4,128)S(1)}, u32[]{:S(2)}, u32[]{:S(2)}) collective-permute-start(f32[4,6,1,4,256]{4,3,2,1,0:T(4,128)S(1)} %get-tuple-element.208), channel_id=1, source_target_pairs={{0,1},{1,0},{2,3},{3,2},{4,5},{5,4},{6,7},{7,6},{8,9},{9,8},{10,11... | collective-permute-start | bytes 294920 | tf_op jit(solution)/shard_map/ppermute | solution.py:25
  55.0 9.0 %collective-permute-start.7 = (f32[4,1,6,4,256]{4,3,2,1,0:T(4,128)S(1)}, f32[4,1,6,4,256]{4,3,2,1,0:T(4,128)S(1)}, u32[]{:S(2)}, u32[]{:S(2)}) collective-permute-start(f32[4,1,6,4,256]{4,3,2,1,0:T(4,128)S(1)} %get-tuple-element.183), channel_id=1, source_target_pairs={{0,6},{2,0},{4,2},{6,4},{1,7},{3,1},{5,3},{7,5},{8,14},{10,8},{12,... | collective-permute-start | bytes 294920 | tf_op jit(solution)/shard_map/ppermute | solution.py:36
  58.7 6.4 %collective-permute-start.6 = (f32[4,1,6,4,256]{4,3,2,1,0:T(4,128)S(1)}, f32[4,1,6,4,256]{4,3,2,1,0:T(4,128)S(1)}, u32[]{:S(2)}, u32[]{:S(2)}) collective-permute-start(f32[4,1,6,4,256]{4,3,2,1,0:T(4,128)S(1)} %get-tuple-element.182), channel_id=1, source_target_pairs={{0,2},{2,4},{4,6},{6,0},{1,3},{3,5},{5,7},{7,1},{8,10},{10,12},{12... | collective-permute-start | bytes 294920 | tf_op jit(solution)/shard_map/ppermute | solution.py:36
  58.8 8.5 %collective-permute-start.4 = (f32[1,6,6,4,256]{4,3,2,1,0:T(4,128)S(1)}, f32[1,6,6,4,256]{4,3,2,1,0:T(4,128)S(1)}, u32[]{:S(2)}, u32[]{:S(2)}) collective-permute-start(f32[1,6,6,4,256]{4,3,2,1,0:T(4,128)S(1)} %pad_maximum_fusion.13), channel_id=1, source_target_pairs={{0,24},{8,0},{16,8},{24,16},{1,25},{9,1},{17,9},{25,17},{2,26},{10... | collective-permute-start | bytes 442376 | tf_op jit(solution)/shard_map/ppermute | solution.py:36
  65.2 15.3 %collective-permute-start.9 = (f32[4,4,1,4,256]{4,3,2,1,0:T(4,128)S(1)}, f32[4,4,1,4,256]{4,3,2,1,0:T(4,128)S(1)}, u32[]{:S(2)}, u32[]{:S(2)}) collective-permute-start(f32[4,4,1,4,256]{4,3,2,1,0:T(4,128)S(1)} %get-tuple-element.211), channel_id=1, source_target_pairs={{0,1},{1,0},{2,3},{3,2},{4,5},{5,4},{6,7},{7,6},{8,9},{9,8},{10,11... | collective-permute-start | bytes 196616 | tf_op jit(solution)/shard_map/ppermute | solution.py:36
  67.2 13.4 %collective-permute-start.8 = (f32[4,4,1,4,256]{4,3,2,1,0:T(4,128)S(1)}, f32[4,4,1,4,256]{4,3,2,1,0:T(4,128)S(1)}, u32[]{:S(2)}, u32[]{:S(2)}) collective-permute-start(f32[4,4,1,4,256]{4,3,2,1,0:T(4,128)S(1)} %get-tuple-element.210), channel_id=1, source_target_pairs={{0,1},{1,0},{2,3},{3,2},{4,5},{5,4},{6,7},{7,6},{8,9},{9,8},{10,11... | collective-permute-start | bytes 196616 | tf_op jit(solution)/shard_map/ppermute | solution.py:36
  140.6 0.8 copy-start.26
  140.6 0.8 copy-start.28
  140.7 0.8 copy-start.30
  140.7 0.8 copy-start.32
  141.4 0.8 copy-start.18
  141.5 0.8 copy-start.20
  141.5 0.8 copy-start.22
  141.5 0.8 copy-start.24
  142.3 0.8 copy-start.10
  142.3 0.8 copy-start.12
  142.3 0.8 copy-start.14
  142.3 0.8 copy-start.16
  143.1 0.8 copy-start.2
  143.1 0.8 copy-start.4
  144.6 4.4 %collective-permute-start.11 = (f32[4,1,4,4,256]{4,3,2,1,0:T(4,128)S(1)}, f32[4,1,4,4,256]{4,3,2,1,0:T(4,128)S(1)}, u32[]{:S(2)}, u32[]{:S(2)}) collective-permute-start(f32[4,1,4,4,256]{4,3,2,1,0:T(4,128)S(1)} %get-tuple-element.297), channel_id=1, source_target_pairs={{2,0},{4,2},{6,4},{0,6},{3,1},{5,3},{7,5},{1,7},{10,8},{12,10},{14... | collective-permute-start | bytes 196616 | tf_op jit(solution)/shard_map/ppermute | solution.py:27
  146.6 12.4 %collective-permute-start.10 = (f32[4,1,4,4,256]{4,3,2,1,0:T(4,128)S(1)}, f32[4,1,4,4,256]{4,3,2,1,0:T(4,128)S(1)}, u32[]{:S(2)}, u32[]{:S(2)}) collective-permute-start(f32[4,1,4,4,256]{4,3,2,1,0:T(4,128)S(1)} %get-tuple-element.296), channel_id=1, source_target_pairs={{0,2},{2,4},{4,6},{6,0},{1,3},{3,5},{5,7},{7,1},{8,10},{10,12},{12... | collective-permute-start | bytes 196616 | tf_op jit(solution)/shard_map/ppermute | solution.py:25
  158.4 11.7 %collective-permute-start.15 = (f32[1,6,6,4,256]{4,3,2,1,0:T(4,128)S(1)}, f32[1,6,6,4,256]{4,3,2,1,0:T(4,128)S(1)}, u32[]{:S(2)}, u32[]{:S(2)}) collective-permute-start(f32[1,6,6,4,256]{4,3,2,1,0:T(4,128)S(1)} %slice.1852), channel_id=1, source_target_pairs={{0,8},{8,16},{16,24},{24,0},{1,9},{9,17},{17,25},{25,1},{2,10},{10... | collective-permute-start | bytes 442376 | tf_op jit(solution)/shard_map/ppermute | solution.py:36
  159.0 5.5 %collective-permute-start.12 = (f32[4,6,1,4,256]{4,3,2,1,0:T(4,128)S(1)}, f32[4,6,1,4,256]{4,3,2,1,0:T(4,128)S(1)}, u32[]{:S(2)}, u32[]{:S(2)}) collective-permute-start(f32[4,6,1,4,256]{4,3,2,1,0:T(4,128)S(1)} %get-tuple-element.205), channel_id=1, source_target_pairs={{1,0},{0,1},{3,2},{2,3},{5,4},{4,5},{7,6},{6,7},{9,8},{8,9},{11,10... | collective-permute-start | bytes 294920 | tf_op jit(solution)/shard_map/ppermute | solution.py:27
  161.3 5.7 %collective-permute-start.13 = (f32[4,6,1,4,256]{4,3,2,1,0:T(4,128)S(1)}, f32[4,6,1,4,256]{4,3,2,1,0:T(4,128)S(1)}, u32[]{:S(2)}, u32[]{:S(2)}) collective-permute-start(f32[4,6,1,4,256]{4,3,2,1,0:T(4,128)S(1)} %get-tuple-element.204), channel_id=1, source_target_pairs={{0,1},{1,0},{2,3},{3,2},{4,5},{5,4},{6,7},{7,6},{8,9},{9,8},{10,11... | collective-permute-start | bytes 294920 | tf_op jit(solution)/shard_map/ppermute | solution.py:25
  167.0 6.6 %collective-permute-start.14 = (f32[1,6,6,4,256]{4,3,2,1,0:T(4,128)S(1)}, f32[1,6,6,4,256]{4,3,2,1,0:T(4,128)S(1)}, u32[]{:S(2)}, u32[]{:S(2)}) collective-permute-start(f32[1,6,6,4,256]{4,3,2,1,0:T(4,128)S(1)} %pad_maximum_fusion.9), channel_id=1, source_target_pairs={{0,24},{8,0},{16,8},{24,16},{1,25},{9,1},{17,9},{25,17},{2,26},{10... | collective-permute-start | bytes 442376 | tf_op jit(solution)/shard_map/ppermute | solution.py:36
  170.3 15.8 %collective-permute-start.17 = (f32[4,1,6,4,256]{4,3,2,1,0:T(4,128)S(1)}, f32[4,1,6,4,256]{4,3,2,1,0:T(4,128)S(1)}, u32[]{:S(2)}, u32[]{:S(2)}) collective-permute-start(f32[4,1,6,4,256]{4,3,2,1,0:T(4,128)S(1)} %get-tuple-element.181), channel_id=1, source_target_pairs={{0,6},{2,0},{4,2},{6,4},{1,7},{3,1},{5,3},{7,5},{8,14},{10,8},{12,... | collective-permute-start | bytes 294920 | tf_op jit(solution)/shard_map/ppermute | solution.py:36
  173.6 12.5 %collective-permute-start.16 = (f32[4,1,6,4,256]{4,3,2,1,0:T(4,128)S(1)}, f32[4,1,6,4,256]{4,3,2,1,0:T(4,128)S(1)}, u32[]{:S(2)}, u32[]{:S(2)}) collective-permute-start(f32[4,1,6,4,256]{4,3,2,1,0:T(4,128)S(1)} %get-tuple-element.180), channel_id=1, source_target_pairs={{0,2},{2,4},{4,6},{6,0},{1,3},{3,5},{5,7},{7,1},{8,10},{10,12},{12... | collective-permute-start | bytes 294920 | tf_op jit(solution)/shard_map/ppermute | solution.py:36
  186.2 5.3 %collective-permute-start.19 = (f32[4,4,1,4,256]{4,3,2,1,0:T(4,128)S(1)}, f32[4,4,1,4,256]{4,3,2,1,0:T(4,128)S(1)}, u32[]{:S(2)}, u32[]{:S(2)}) collective-permute-start(f32[4,4,1,4,256]{4,3,2,1,0:T(4,128)S(1)} %get-tuple-element.207), channel_id=1, source_target_pairs={{0,1},{1,0},{2,3},{3,2},{4,5},{5,4},{6,7},{7,6},{8,9},{9,8},{10,11... | collective-permute-start | bytes 196616 | tf_op jit(solution)/shard_map/ppermute | solution.py:36
  188.6 4.3 %collective-permute-start.18 = (f32[4,4,1,4,256]{4,3,2,1,0:T(4,128)S(1)}, f32[4,4,1,4,256]{4,3,2,1,0:T(4,128)S(1)}, u32[]{:S(2)}, u32[]{:S(2)}) collective-permute-start(f32[4,4,1,4,256]{4,3,2,1,0:T(4,128)S(1)} %get-tuple-element.206), channel_id=1, source_target_pairs={{0,1},{1,0},{2,3},{3,2},{4,5},{5,4},{6,7},{7,6},{8,9},{9,8},{10,11... | collective-permute-start | bytes 196616 | tf_op jit(solution)/shard_map/ppermute | solution.py:36
  255.9 4.5 %collective-permute-start.21 = (f32[4,1,4,4,256]{4,3,2,1,0:T(4,128)S(1)}, f32[4,1,4,4,256]{4,3,2,1,0:T(4,128)S(1)}, u32[]{:S(2)}, u32[]{:S(2)}) collective-permute-start(f32[4,1,4,4,256]{4,3,2,1,0:T(4,128)S(1)} %get-tuple-element.235), channel_id=1, source_target_pairs={{2,0},{4,2},{6,4},{0,6},{3,1},{5,3},{7,5},{1,7},{10,8},{12,10},{14... | collective-permute-start | bytes 196616 | tf_op jit(solution)/shard_map/ppermute | solution.py:27
  257.9 12.2 %collective-permute-start.20 = (f32[4,1,4,4,256]{4,3,2,1,0:T(4,128)S(1)}, f32[4,1,4,4,256]{4,3,2,1,0:T(4,128)S(1)}, u32[]{:S(2)}, u32[]{:S(2)}) collective-permute-start(f32[4,1,4,4,256]{4,3,2,1,0:T(4,128)S(1)} %get-tuple-element.234), channel_id=1, source_target_pairs={{0,2},{2,4},{4,6},{6,0},{1,3},{3,5},{5,7},{7,1},{8,10},{10,12},{12... | collective-permute-start | bytes 196616 | tf_op jit(solution)/shard_map/ppermute | solution.py:25
  269.8 11.5 %collective-permute-start.25 = (f32[1,6,6,4,256]{4,3,2,1,0:T(4,128)S(1)}, f32[1,6,6,4,256]{4,3,2,1,0:T(4,128)S(1)}, u32[]{:S(2)}, u32[]{:S(2)}) collective-permute-start(f32[1,6,6,4,256]{4,3,2,1,0:T(4,128)S(1)} %slice.1910), channel_id=1, source_target_pairs={{0,8},{8,16},{16,24},{24,0},{1,9},{9,17},{17,25},{25,1},{2,10},{10... | collective-permute-start | bytes 442376 | tf_op jit(solution)/shard_map/ppermute | solution.py:36
  270.2 5.5 %collective-permute-start.22 = (f32[4,6,1,4,256]{4,3,2,1,0:T(4,128)S(1)}, f32[4,6,1,4,256]{4,3,2,1,0:T(4,128)S(1)}, u32[]{:S(2)}, u32[]{:S(2)}) collective-permute-start(f32[4,6,1,4,256]{4,3,2,1,0:T(4,128)S(1)} %get-tuple-element.201), channel_id=1, source_target_pairs={{1,0},{0,1},{3,2},{2,3},{5,4},{4,5},{7,6},{6,7},{9,8},{8,9},{11,10... | collective-permute-start | bytes 294920 | tf_op jit(solution)/shard_map/ppermute | solution.py:27
  272.5 5.7 %collective-permute-start.23 = (f32[4,6,1,4,256]{4,3,2,1,0:T(4,128)S(1)}, f32[4,6,1,4,256]{4,3,2,1,0:T(4,128)S(1)}, u32[]{:S(2)}, u32[]{:S(2)}) collective-permute-start(f32[4,6,1,4,256]{4,3,2,1,0:T(4,128)S(1)} %get-tuple-element.200), channel_id=1, source_target_pairs={{0,1},{1,0},{2,3},{3,2},{4,5},{5,4},{6,7},{7,6},{8,9},{9,8},{10,11... | collective-permute-start | bytes 294920 | tf_op jit(solution)/shard_map/ppermute | solution.py:25
  278.2 6.5 %collective-permute-start.24 = (f32[1,6,6,4,256]{4,3,2,1,0:T(4,128)S(1)}, f32[1,6,6,4,256]{4,3,2,1,0:T(4,128)S(1)}, u32[]{:S(2)}, u32[]{:S(2)}) collective-permute-start(f32[1,6,6,4,256]{4,3,2,1,0:T(4,128)S(1)} %pad_maximum_fusion.5), channel_id=1, source_target_pairs={{0,24},{8,0},{16,8},{24,16},{1,25},{9,1},{17,9},{25,17},{2,26},{10... | collective-permute-start | bytes 442376 | tf_op jit(solution)/shard_map/ppermute | solution.py:36
  281.5 15.8 %collective-permute-start.27 = (f32[4,1,6,4,256]{4,3,2,1,0:T(4,128)S(1)}, f32[4,1,6,4,256]{4,3,2,1,0:T(4,128)S(1)}, u32[]{:S(2)}, u32[]{:S(2)}) collective-permute-start(f32[4,1,6,4,256]{4,3,2,1,0:T(4,128)S(1)} %get-tuple-element.179), channel_id=1, source_target_pairs={{0,6},{2,0},{4,2},{6,4},{1,7},{3,1},{5,3},{7,5},{8,14},{10,8},{12,... | collective-permute-start | bytes 294920 | tf_op jit(solution)/shard_map/ppermute | solution.py:36
  284.8 12.5 %collective-permute-start.26 = (f32[4,1,6,4,256]{4,3,2,1,0:T(4,128)S(1)}, f32[4,1,6,4,256]{4,3,2,1,0:T(4,128)S(1)}, u32[]{:S(2)}, u32[]{:S(2)}) collective-permute-start(f32[4,1,6,4,256]{4,3,2,1,0:T(4,128)S(1)} %get-tuple-element.178), channel_id=1, source_target_pairs={{0,2},{2,4},{4,6},{6,0},{1,3},{3,5},{5,7},{7,1},{8,10},{10,12},{12... | collective-permute-start | bytes 294920 | tf_op jit(solution)/shard_map/ppermute | solution.py:36
  297.4 5.3 %collective-permute-start.29 = (f32[4,4,1,4,256]{4,3,2,1,0:T(4,128)S(1)}, f32[4,4,1,4,256]{4,3,2,1,0:T(4,128)S(1)}, u32[]{:S(2)}, u32[]{:S(2)}) collective-permute-start(f32[4,4,1,4,256]{4,3,2,1,0:T(4,128)S(1)} %get-tuple-element.203), channel_id=1, source_target_pairs={{0,1},{1,0},{2,3},{3,2},{4,5},{5,4},{6,7},{7,6},{8,9},{9,8},{10,11... | collective-permute-start | bytes 196616 | tf_op jit(solution)/shard_map/ppermute | solution.py:36
  299.8 4.3 %collective-permute-start.28 = (f32[4,4,1,4,256]{4,3,2,1,0:T(4,128)S(1)}, f32[4,4,1,4,256]{4,3,2,1,0:T(4,128)S(1)}, u32[]{:S(2)}, u32[]{:S(2)}) collective-permute-start(f32[4,4,1,4,256]{4,3,2,1,0:T(4,128)S(1)} %get-tuple-element.202), channel_id=1, source_target_pairs={{0,1},{1,0},{2,3},{3,2},{4,5},{5,4},{6,7},{7,6},{8,9},{9,8},{10,11... | collective-permute-start | bytes 196616 | tf_op jit(solution)/shard_map/ppermute | solution.py:36
  (3 other events, 2.2 us)
where the time goes:
time: 355 us; the launch traced here: 349 us
  other arithmetic  159 us (45%)
  blocking collectives  118 us (33%)
  starting transfers between devices  37.1 us (10%)
  waiting for transfers between devices  17.9 us (5%)
  local copies, waits for them, and re-layouts  13.9 us (4%)
    psum x3, blocking collectives, two_products(): lax.psum((jnp.sum(residual * residual, axis=(0, 1, 2, 3)), jnp.sum(residu...  118 us
    add x162, other arithmetic, block_apply(): total = term if total is None else total + term  117 us
    add x3, other arithmetic, operate(): spilled = spilled + jnp.pad(hop_back(coupled[bond_index], vector), placed)  25.9 us
    ppermute x18, starting transfers between devices, shifted(): lax.ppermute(value, axis, [(i, (i + by) % peers) for i in range(peers)])  20.5 us
    reduce_sum x3, other arithmetic, two_products(): jnp.sum(residual * image, axis=(0, 1, 2, 3))  11.9 us
    ppermute x6, starting transfers between devices, extended_2(): lax.ppermute(head, axis, [((i + 1) % count, i) for i in range(count)])  11.6 us
    ppermute x6, waiting for transfers between devices, extended_2(): lax.ppermute(head, axis, [((i + 1) % count, i) for i in range(count)])  9.28 us
    slice x1, local copies, waits for them, and re-layouts, operate(): coupled[bond_index]  8.42 us
  transfers between devices with their start and end apart: 30, of which 12 were waited for; matrix products, arithmetic and copies ran while one was open for 33% of the time, Pallas kernels for 0%

commit v1 on v0

v1 whole, which is shorter than its diff:
```python
import functools

import jax
import jax.numpy as jnp
from jax import lax
from jax.experimental import pallas as pl
from jax.experimental.pallas import tpu as pltpu
from jax.sharding import PartitionSpec as P

ITERS = 3
LANES = 128
ROWS = 16
ALL = ("gx", "gy", "gz")

half_offsets = [
    (first, second, third)
    for first in (-1, 0, 1)
    for second in (-1, 0, 1)
    for third in (-1, 0, 1)
    if (first, second, third) > (0, 0, 0)
]
ONSITE = len(half_offsets)


def shifted(value, axis, by):
    peers = lax.axis_size(axis)
    return lax.ppermute(value, axis, [(i, (i + by) % peers) for i in range(peers)])


def chip_shifted(value, by):
    peers = lax.axis_size("gx")
    return lax.ppermute(value, "gx", [(i, (i + 2 * by) % peers) for i in range(peers)])


def core_swapped(value):
    peers = lax.axis_size("gx")
    return lax.ppermute(value, "gx", [(i, i ^ 1) for i in range(peers)])


def gather_blocks(block):
    count_y, count_z, chips = lax.axis_size("gy"), lax.axis_size("gz"), lax.axis_size("gx") // 2
    along_y = [block] + [shifted(block, "gy", by) for by in range(1, count_y)]
    first = jnp.stack(along_y[: count_y // 2])
    second = jnp.stack(along_y[count_y // 2 :])
    first = jnp.stack([first] + [chip_shifted(first, by) for by in range(1, chips)])
    second = jnp.stack([second] + [shifted(second, "gz", by) for by in range(1, count_z)])
    first = jnp.stack([first] + [shifted(first, "gz", by) for by in range(1, count_z)])
    second = jnp.stack([second] + [chip_shifted(second, by) for by in range(1, chips)])
    own = jnp.concatenate([first.reshape((-1,) + block.shape), second.reshape((-1,) + block.shape)])
    return own, core_swapped(own)


def turn_groups(parts, group, seg):
    count = len(parts)
    bit = 1
    while bit < count:
        high = (group & bit) != 0
        turned = []
        for index in range(count):
            other = parts[index ^ bit]
            if index & bit:
                turned.append(jnp.where(high, parts[index], pltpu.roll(other, LANES - bit * seg, 1)))
            else:
                turned.append(jnp.where(high, pltpu.roll(other, bit * seg, 1), parts[index]))
        parts = turned
        bit *= 2
    return parts


def cg_kernel(sizes, columns_ref, own_ref, other_ref, shift_ref, out_ref, coef, field, image, answer, residual, ahead):
    count_x, count_y, count_z, lx, ly, lz, orbitals = sizes
    seg = lx * lz
    per = LANES // seg
    width = count_x * count_z * seg
    high = count_y * ly
    chips = count_x // 2
    tiles = width // LANES
    halves = ly * orbitals // per
    group = lax.broadcasted_iota(jnp.int32, (1, LANES), 1) // seg
    lane = lax.broadcasted_iota(jnp.int32, (1, width), 1)
    at_z, at_x, at_gz = lane % lz, (lane // lz) % lx, (lane // seg) % count_z
    step_x = seg * count_z - (lx - 1) * lz
    step_z = seg - lz + 1
    wrap_z = (count_z - 1) * seg + lz - 1

    def roll(value, by):
        return pltpu.roll(value, by % width, 1)

    def from_next_z(value):
        return jnp.where(at_z < lz - 1, roll(value, -1), jnp.where(at_gz < count_z - 1, roll(value, -step_z), roll(value, wrap_z)))

    def from_last_z(value):
        return jnp.where(at_z > 0, roll(value, 1), jnp.where(at_gz > 0, roll(value, step_z), roll(value, -wrap_z)))

    def from_next_x(value):
        return jnp.where(at_x < lx - 1, roll(value, -lz), roll(value, -step_x))

    def from_last_x(value):
        return jnp.where(at_x > 0, roll(value, lz), roll(value, step_x))

    def device_of(source, gy):
        return ((source // count_z) * count_y + gy) * count_z + source % count_z

    for gy in range(count_y):
        for tile in range(tiles):
            for half in range(halves):
                parts = [
                    columns_ref[device_of(tile * per + p, gy), :, half * LANES : (half + 1) * LANES]
                    for p in range(per)
                ]
                for g, value in enumerate(turn_groups(parts, group, seg)):
                    y, orb = divmod(half * per + g, orbitals)
                    field[gy * ly + y, orb, :, tile * LANES : (tile + 1) * LANES] = value

    my_x, my_y, my_z = lax.axis_index("gx"), lax.axis_index("gy"), lax.axis_index("gz")
    my_chip, my_core = my_x // 2, my_x % 2
    half_y = count_y // 2

    def fill(gy, carry):
        away = lax.rem(my_y - gy + count_y, count_y)
        near = away < half_y
        for tile in range(tiles):
            slots, cores = [], []
            for p in range(per):
                gx, gz = divmod(tile * per + p, count_z)
                across = lax.rem(my_chip - gx // 2 + chips, chips)
                up = lax.rem(my_z - gz + count_z, count_z)
                slots.append(
                    jnp.where(
                        near,
                        (up * chips + across) * half_y + away,
                        (chips * count_z + across * count_z + up) * half_y + away - half_y,
                    )
                )
                cores.append(gx % 2 == my_core)
            for part in range(orbitals * orbitals * ly // per):
                lanes = slice(part * LANES, (part + 1) * LANES)
                parts = [
                    jnp.where(core, own_ref[slot, :, lanes], other_ref[slot, :, lanes])
                    for slot, core in zip(slots, cores)
                ]
                for g, value in enumerate(turn_groups(parts, group, seg)):
                    pair, y = divmod(part * per + g, ly)
                    coef[gy * ly + y, pair, :, tile * LANES : (tile + 1) * LANES] = value
        return carry

    lax.fori_loop(0, count_y, fill, 0)

    shift = shift_ref[...]
    zero = jnp.zeros(field.shape[2:], jnp.float32)

    def start(y, total):
        for orb in range(orbitals):
            value = field[y, orb]
            residual[y, orb] = value
            total = total + value * value
        return total

    norm_now = jnp.sum(lax.fori_loop(0, high, start, zero), axis=1, keepdims=True)

    directions = ((0, 1), (0, -1), (1, 0), (1, 1), (1, -1))

    def spread(y, carry):
        for orb in range(orbitals):
            value = field[y, orb]
            above, below = from_next_z(value), from_last_z(value)
            ahead[0, y, orb] = above
            ahead[1, y, orb] = below
            ahead[2, y, orb] = from_next_x(value)
            ahead[3, y, orb] = from_next_x(above)
            ahead[4, y, orb] = from_next_x(below)
        return carry

    def apply(y, total):
        rows = {0: y, 1: lax.rem(y + 1, high), -1: lax.rem(y + high - 1, high)}

        def factor(row, i, j, k):
            return coef[row, i * orbitals + j, k : k + 1, :]

        here = [field[y, orb] for orb in range(orbitals)]
        result = [shift * value for value in here]
        for j in range(orbitals):
            for i in range(orbitals):
                result[i] = result[i] + factor(y, i, j, ONSITE) * here[j]
        for k, (first, second, third) in enumerate(half_offsets):
            for j in range(orbitals):
                if (first, third) == (0, 0):
                    value = field[rows[second], j]
                else:
                    value = ahead[directions.index((first, third)), rows[second], j]
                for i in range(orbitals):
                    result[i] = result[i] + factor(y, i, j, k) * value
        landing = {}
        for first, third in ((0, 0), (0, 1), (0, -1), (1, 0), (1, 1), (1, -1)):
            sums = [None] * orbitals
            for k, offset in enumerate(half_offsets):
                if (offset[0], offset[2]) != (first, third):
                    continue
                row = rows[-offset[1]]
                for j in range(orbitals):
                    value = field[row, j]
                    for i in range(orbitals):
                        term = factor(row, j, i, k) * value
                        sums[i] = term if sums[i] is None else sums[i] + term
            if third == 1:
                sums = [from_last_z(value) for value in sums]
            elif third == -1:
                sums = [from_next_z(value) for value in sums]
            landing[first] = [a + b for a, b in zip(landing[first], sums)] if first in landing else sums
        for i in range(orbitals):
            value = result[i] + landing[0][i] + from_last_x(landing[1][i])
            image[y, i] = value
            total = total + value * here[i]
        return total

    for iteration in range(ITERS):
        lax.fori_loop(0, high, spread, 0)
        product = jnp.sum(lax.fori_loop(0, high, apply, zero), axis=1, keepdims=True)
        alpha = norm_now / product

        def advance(y, total):
            for orb in range(orbitals):
                move = alpha * field[y, orb]
                answer[y, orb] = move if iteration == 0 else answer[y, orb] + move
                value = residual[y, orb] - alpha * image[y, orb]
                residual[y, orb] = value
                total = total + value * value
            return total

        total = lax.fori_loop(0, high, advance, zero)
        if iteration + 1 < ITERS:
            norm_next = jnp.sum(total, axis=1, keepdims=True)
            ratio = norm_next / norm_now

            def turn(y, carry):
                for orb in range(orbitals):
                    field[y, orb] = residual[y, orb] + ratio * field[y, orb]
                return carry

            lax.fori_loop(0, high, turn, 0)
            norm_now = norm_next

    for which, source in enumerate((answer, residual)):
        for gy in range(count_y):
            for tile in range(tiles):
                for half in range(halves):
                    parts = []
                    for g in range(per):
                        y, orb = divmod(half * per + g, orbitals)
                        parts.append(source[gy * ly + y, orb, :, tile * LANES : (tile + 1) * LANES])
                    for p, value in enumerate(turn_groups(parts, group, seg)):
                        out_ref[device_of(tile * per + p, gy), which, :, half * LANES : (half + 1) * LANES] = value


def block_kernel(bonds_ref, open_ref, onsite_ref, levels_ref, out_ref, rows):
    orbitals, lx, ly, lz = levels_ref.shape
    bonds = bonds_ref.shape[-1]
    rows[...] = jnp.zeros_like(rows)
    eye = (
        lax.broadcasted_iota(jnp.int32, (lz, lz), 0) == lax.broadcasted_iota(jnp.int32, (lz, lz), 1)
    ).astype(jnp.float32)
    for i in range(orbitals):
        for j in range(orbitals):
            for x in range(lx):
                local = 0.5 * (onsite_ref[i, j, x] + onsite_ref[j, i, x])
                if i == j:
                    local = local + levels_ref[i, x]
                for y in range(ly):
                    row = (((i * orbitals + j) * ly + y) * lx + x) * lz
                    mask = open_ref[x * ly + y].astype(jnp.float32)
                    rows[row : row + lz, :bonds] = bonds_ref[((i * orbitals + j) * lx + x) * ly + y] * mask
                    rows[row : row + lz, bonds : bonds + lz] = eye * local[y : y + 1, :]
    turned = jnp.transpose(rows[...])
    last = jnp.sum(turned[bonds : bonds + lz], axis=0, keepdims=True)
    place = lax.broadcasted_iota(jnp.int32, out_ref.shape, 0)
    out_ref[...] = jnp.where(place < bonds, turned[:ROWS], jnp.where(place == bonds, last, 0.0))


def pack_kernel(field_ref, out_ref, rows):
    lx, ly, lz, orbitals, _ = field_ref.shape
    for x in range(lx):
        for y in range(ly):
            for z in range(lz):
                base = y * orbitals * lx * lz + x * lz + z
                for tile in range(rows.shape[0]):
                    lanes = slice(tile * LANES, (tile + 1) * LANES)
                    rows[tile, pl.ds(base, orbitals, stride=lx * lz), :] = field_ref[x, y, z, :, lanes]
    for tile in range(rows.shape[0]):
        out_ref[tile * LANES : (tile + 1) * LANES, :] = jnp.transpose(rows[tile])


def unpack_kernel(back_ref, answer_ref, residual_ref, rows):
    lx, ly, lz, orbitals, columns = answer_ref.shape
    for which, out_ref in enumerate((answer_ref, residual_ref)):
        turned = jnp.transpose(back_ref[:, which].reshape(columns, -1))
        for tile in range(rows.shape[1]):
            rows[which, tile] = turned[:, tile * LANES : (tile + 1) * LANES]
        for x in range(lx):
            for y in range(ly):
                for z in range(lz):
                    base = y * orbitals * lx * lz + x * lz + z
                    for tile in range(rows.shape[1]):
                        lanes = slice(tile * LANES, (tile + 1) * LANES)
                        out_ref[x, y, z, :, lanes] = rows[which, tile, pl.ds(base, orbitals, stride=lx * lz), :]


def per_device(right_side, bond_blocks, bond_open, onsite_blocks, orbital_levels, column_shift):
    lx, ly, lz, orbitals, columns = right_side.shape
    count_x, count_y, count_z = (lax.axis_size(axis) for axis in ALL)
    devices = count_x * count_y * count_z
    own_columns = columns // devices
    padded = -(-own_columns // 8) * 8
    seg = lx * lz
    width = count_x * count_z * seg
    high = count_y * ly
    assert LANES % seg == 0 and width % LANES == 0 and count_x % 2 == 0 and count_y % 2 == 0
    assert (ly * orbitals) % (LANES // seg) == 0 and columns % devices == 0

    atoms = lx * ly * lz
    bonds = bond_blocks.shape[0]
    vmem = pl.BlockSpec(memory_space=pltpu.VMEM)
    block = pl.pallas_call(
        block_kernel,
        out_shape=jax.ShapeDtypeStruct((ROWS, orbitals * orbitals * atoms), jnp.float32),
        in_specs=[vmem] * 4,
        out_specs=vmem,
        scratch_shapes=[pltpu.VMEM((orbitals * orbitals * atoms, LANES), jnp.float32)],
        name="block",
    )(
        jnp.transpose(bond_blocks, (1, 2, 3, 4, 5, 0)).reshape(-1, lz, bonds),
        jnp.transpose(bond_open, (1, 2, 3, 0)).reshape(-1, lz, bonds),
        onsite_blocks,
        orbital_levels,
    )
    own, other = gather_blocks(block)

    packed = pl.pallas_call(
        pack_kernel,
        out_shape=jax.ShapeDtypeStruct((columns, orbitals * atoms), jnp.float32),
        in_specs=[vmem],
        out_specs=vmem,
        scratch_shapes=[pltpu.VMEM((columns // LANES, orbitals * atoms, LANES), jnp.float32)],
        name="pack",
    )(right_side)
    packed = packed.reshape(devices, own_columns, orbitals * atoms)
    received = lax.all_to_all(packed, ALL, 0, 0, tiled=True)
    index = (lax.axis_index("gx") * count_y + lax.axis_index("gy")) * count_z + lax.axis_index("gz")
    shift = lax.dynamic_slice_in_dim(column_shift, index * own_columns, own_columns)
    if padded != own_columns:
        received = jnp.pad(received, ((0, 0), (0, padded - own_columns), (0, 0)))
        shift = jnp.pad(shift, (0, padded - own_columns))
    shift = jnp.broadcast_to(shift[:, None], (padded, width))

    sizes = (count_x, count_y, count_z, lx, ly, lz, orbitals)
    state = pltpu.VMEM((high, orbitals, padded, width), jnp.float32)
    out = pl.pallas_call(
        functools.partial(cg_kernel, sizes),
        out_shape=jax.ShapeDtypeStruct((devices, 2, padded, ly * orbitals * seg), jnp.float32),
        in_specs=[pl.BlockSpec(memory_space=pltpu.VMEM)] * 4,
        out_specs=pl.BlockSpec(memory_space=pltpu.VMEM),
        scratch_shapes=[
            pltpu.VMEM((high, orbitals * orbitals, ROWS, width), jnp.float32),
            state,
            state,
            state,
            state,
            pltpu.VMEM((5, high, orbitals, padded, width), jnp.float32),
        ],
        compiler_params=pltpu.CompilerParams(vmem_limit_bytes=56 * 1024 * 1024),
        name="cg",
    )(received, own, other, shift)
    if padded != own_columns:
        out = out[:, :, :own_columns]
    back = lax.all_to_all(out, ALL, 0, 0, tiled=True)
    shape = jax.ShapeDtypeStruct(right_side.shape, jnp.float32)
    return tuple(
        pl.pallas_call(
            unpack_kernel,
            out_shape=(shape, shape),
            in_specs=[vmem],
            out_specs=(vmem, vmem),
            scratch_shapes=[pltpu.VMEM((2, columns // LANES, orbitals * atoms, LANES), jnp.float32)],
            name="unpack",
        )(back)
    )


def solution(mesh):
    placed = (
        P("gx", "gy", "gz", None, None),
        P(None, None, None, "gx", "gy", "gz"),
        P(None, "gx", "gy", "gz"),
        P(None, None, "gx", "gy", "gz"),
        P(None, "gx", "gy", "gz"),
        P(),
    )
    return jax.shard_map(
        per_device,
        mesh=mesh,
        in_specs=placed,
        out_specs=(P("gx", "gy", "gz", None, None), P("gx", "gy", "gz", None, None)),
        check_vma=False,
    )
```

time: 355 us -> 95.3 us (0.27); the launches traced: 349 us -> 94.9 us
  other arithmetic: 159 us -> 0.31 us
  blocking collectives: 118 us -> 19.5 us
  Pallas kernels: 0 us -> 33.3 us
  starting transfers between devices: 37.1 us -> 16.4 us
  local copies, waits for them, and re-layouts: 13.9 us -> 1.84 us
  waiting for transfers between devices: 17.9 us -> 22.8 us
    add x171 -> x0, other arithmetic: 143 us -> none  [the longest x162 117 us: block_apply(): total = term if total is None else total + term]
    psum x3 -> x0, blocking collectives: 118 us -> none  [two_products(): lax.psum((jnp.sum(residual * residual, axis=(0, 1, 2, 3)), jnp.sum(residu...]
    pallas_call x0 -> x4, Pallas kernels: none -> 33.3 us  [the longest x1 27 us: per_device(): pl.pallas_call(functools.partial(cg_kernel, sizes), out_shape=jax.ShapeDt...]
    all_to_all x0 -> x1, blocking collectives: none -> 19.5 us  [per_device(): back = lax.all_to_all(out, ALL, 0, 0, tiled=True)]
    ppermute x12 -> x3, starting transfers between devices: 16.6 us -> 3.18 us  [the longest x2 3.11 us: chip_shifted(): lax.ppermute(value, 'gx', [(i, (i + 2 * by) % peers) for i in range(peers)])]
    reduce_sum x3 -> x0, other arithmetic: 11.9 us -> none  [two_products(): jnp.sum(residual * image, axis=(0, 1, 2, 3))]
    ppermute x18 -> x5, starting transfers between devices: 20.5 us -> 9.26 us  [shifted(): lax.ppermute(value, axis, [(i, (i + by) % peers) for i in range(peers)])]
    slice x14 -> x0, local copies, waits for them, and re-layouts: 10.1 us -> none  [the longest x1 8.42 us: operate(): coupled[bond_index]]
  transfers between devices with their start and end apart: 30 -> 9, of which waited for: 12 -> 6; matrix products, arithmetic and copies ran while one was open for 33% -> 0% of each run, Pallas kernels for 0% -> 2%
where the time goes in v1:
time: 95.3 us; the launch traced here: 94.9 us
  Pallas kernels  33.3 us (35%)
  waiting for transfers between devices  22.8 us (24%)
  blocking collectives  19.5 us (20%)
  starting transfers between devices  16.4 us (17%)
  local copies, waits for them, and re-layouts  1.84 us (2%)
    pallas_call x1, Pallas kernels, per_device(): pl.pallas_call(functools.partial(cg_kernel, sizes), out_shape=jax.ShapeDt...  27 us
    all_to_all x1, blocking collectives, per_device(): back = lax.all_to_all(out, ALL, 0, 0, tiled=True)  19.5 us
    all_to_all x1, waiting for transfers between devices, per_device(): received = lax.all_to_all(packed, ALL, 0, 0, tiled=True)  9.68 us
    ppermute x5, starting transfers between devices, shifted(): lax.ppermute(value, axis, [(i, (i + by) % peers) for i in range(peers)])  9.26 us
    ppermute x5, waiting for transfers between devices, shifted(): lax.ppermute(value, axis, [(i, (i + by) % peers) for i in range(peers)])  9.07 us
    ppermute x2, waiting for transfers between devices, chip_shifted(): lax.ppermute(value, 'gx', [(i, (i + 2 * by) % peers) for i in range(peers)])  4.05 us
    all_to_all x1, starting transfers between devices, per_device(): received = lax.all_to_all(packed, ALL, 0, 0, tiled=True)  3.95 us
    ppermute x2, starting transfers between devices, chip_shifted(): lax.ppermute(value, 'gx', [(i, (i + 2 * by) % peers) for i in range(peers)])  3.11 us
  transfers between devices with their start and end apart: 9, of which 6 were waited for; matrix products, arithmetic and copies ran while one was open for 0% of the time, Pallas kernels for 2%

profile of v1, /device:TPU:0, one launch (start us, length us, event | category | flops | bytes accessed | tf_op | source)
XLA Modules:
  0.0 94.9 jit_solution(1551246392352756975)
XLA Ops:
  0.6 2.2 %block.1 = f32[16,1024]{1,0:T(8,128)} custom-call(f32[256,4,13]{2,1,0:T(4,128)} %bitcast.28, s32[16,4,13]{2,1,0:T(4,128)} %bitcast.37, f32[4,4,4,4,4]{4,3,2,1,0:T(4,128)} %onsite_ref.1, f32[4,4,4,4]{3,2,1,0:T(4,128)} %levels_ref.1), custom_call_target="tpu_custom_call" | custom-call | tf_op jit(solution)/shard_map/block/pallas_call | solution.py:322
  2.8 5.1 %collective-permute-start.4 = (f32[16,1024]{1,0:T(8,128)}, f32[16,1024]{1,0:T(8,128)S(1)}, u32[]{:S(2)}, u32[]{:S(2)}) collective-permute-start(f32[16,1024]{1,0:T(8,128)} %block.1), channel_id=1, source_target_pairs={{0,6},{2,0},{4,2},{6,4},{1,7},{3,1},{5,3},{7,5},{8,14},{10,8},{12,... | collective-permute-start | bytes 196616 | tf_op jit(solution)/shard_map/ppermute | solution.py:27
  7.9 0.0 collective-permute-start.3
  7.9 1.0 %collective-permute-start = (f32[16,1024]{1,0:T(8,128)}, f32[16,1024]{1,0:T(8,128)S(1)}, u32[]{:S(2)}, u32[]{:S(2)}) collective-permute-start(f32[16,1024]{1,0:T(8,128)} %block.1), channel_id=1, source_target_pairs={{0,2},{2,4},{4,6},{6,0},{1,3},{3,5},{5,7},{7,1},{8,10},{10,12},{12... | collective-permute-start | bytes 196616 | tf_op jit(solution)/shard_map/ppermute | solution.py:27
  8.9 1.8 %collective-permute-done.4 = f32[16,1024]{1,0:T(8,128)S(1)} collective-permute-done((f32[16,1024]{1,0:T(8,128)}, f32[16,1024]{1,0:T(8,128)S(1)}, u32[]{:S(2)}, u32[]{:S(2)}) %collective-permute-start.4) | collective-permute-done | bytes 65568 | tf_op jit(solution)/shard_map/ppermute | solution.py:27
  10.7 3.9 %collective-permute-done.3 = f32[16,1024]{1,0:T(8,128)S(1)} collective-permute-done((f32[16,1024]{1,0:T(8,128)}, f32[16,1024]{1,0:T(8,128)S(1)}, u32[]{:S(2)}, u32[]{:S(2)}) %collective-permute-start.3) | collective-permute-done | bytes 65568 | tf_op jit(solution)/shard_map/ppermute | solution.py:27
  14.6 0.0 copy-start.3
  14.6 1.6 %collective-permute-start.5 = (f32[2,16,1024]{2,1,0:T(8,128)S(1)}, f32[2,16,1024]{2,1,0:T(8,128)S(1)}, u32[]{:S(2)}, u32[]{:S(2)}) collective-permute-start(f32[2,16,1024]{2,1,0:T(8,128)S(1)} %get-tuple-element.9), channel_id=1, source_target_pairs={{0,1},{1,0},{2,3},{3,2},{4,5},{5,4},{6,7},{7,6},{8,9},{9,8},{10,11... | collective-permute-start | bytes 393224 | tf_op jit(solution)/shard_map/ppermute | solution.py:27
  16.2 0.0 collective-permute-done
  16.2 0.0 copy-done.3
  16.2 1.6 %collective-permute-start.1 = (f32[2,16,1024]{2,1,0:T(8,128)S(1)}, f32[2,16,1024]{2,1,0:T(8,128)S(1)}, u32[]{:S(2)}, u32[]{:S(2)}) collective-permute-start(f32[2,16,1024]{2,1,0:T(8,128)S(1)} %get-tuple-element.7), channel_id=1, source_target_pairs={{0,16},{8,24},{16,0},{24,8},{1,17},{9,25},{17,1},{25,9},{2,18},{10... | collective-permute-start | bytes 393224 | tf_op jit(solution)/shard_map/ppermute | solution.py:32
  17.8 2.1 %collective-permute-done.5 = f32[2,16,1024]{2,1,0:T(8,128)S(1)} collective-permute-done((f32[2,16,1024]{2,1,0:T(8,128)S(1)}, f32[2,16,1024]{2,1,0:T(8,128)S(1)}, u32[]{:S(2)}, u32[]{:S(2)}) %collective-permute-start.5) | collective-permute-done | bytes 131104 | tf_op jit(solution)/shard_map/ppermute | solution.py:27
  20.0 1.6 %collective-permute-start.6 = (f32[2,2,16,1024]{3,2,1,0:T(8,128)S(1)}, f32[2,2,16,1024]{3,2,1,0:T(8,128)S(1)}, u32[]{:S(2)}, u32[]{:S(2)}) collective-permute-start(f32[2,2,16,1024]{3,2,1,0:T(8,128)S(1)} %get-tuple-element.5), channel_id=1, source_target_pairs={{0,16},{8,24},{16,0},{24,8},{1,17},{9,25},{17,1},{25,9},{2,18},{10... | collective-permute-start | bytes 786440 | tf_op jit(solution)/shard_map/ppermute | solution.py:32
  21.5 0.0 collective-permute-done.1
  21.6 1.6 %collective-permute-start.2 = (f32[2,2,16,1024]{3,2,1,0:T(8,128)S(1)}, f32[2,2,16,1024]{3,2,1,0:T(8,128)S(1)}, u32[]{:S(2)}, u32[]{:S(2)}) collective-permute-start(f32[2,2,16,1024]{3,2,1,0:T(8,128)S(1)} %get-tuple-element.3), channel_id=1, source_target_pairs={{0,1},{1,0},{2,3},{3,2},{4,5},{5,4},{6,7},{7,6},{8,9},{9,8},{10,11... | collective-permute-start | bytes 786440 | tf_op jit(solution)/shard_map/ppermute | solution.py:27
  23.2 4.0 %collective-permute-done.6 = f32[2,2,16,1024]{3,2,1,0:T(8,128)S(1)} collective-permute-done((f32[2,2,16,1024]{3,2,1,0:T(8,128)S(1)}, f32[2,2,16,1024]{3,2,1,0:T(8,128)S(1)}, u32[]{:S(2)}, u32[]{:S(2)}) %collective-permute-start.6) | collective-permute-done | bytes 262176 | tf_op jit(solution)/shard_map/ppermute | solution.py:32
  27.3 1.3 %collective-permute-done.2 = f32[2,2,16,1024]{3,2,1,0:T(8,128)S(1)} collective-permute-done((f32[2,2,16,1024]{3,2,1,0:T(8,128)S(1)}, f32[2,2,16,1024]{3,2,1,0:T(8,128)S(1)}, u32[]{:S(2)}, u32[]{:S(2)}) %collective-permute-start.2) | collective-permute-done | bytes 262176 | tf_op jit(solution)/shard_map/ppermute | solution.py:27
  28.6 0.1 pad_maximum_fusion.own_ref
  28.7 0.0 copy-start
  28.7 0.1 collective-permute-start.7
  28.8 2.1 %pack.1 = f32[256,256]{1,0:T(8,128)} custom-call(f32[4,4,4,4,256]{4,3,2,1,0:T(4,128)} %field_ref.1), custom_call_target="tpu_custom_call" | custom-call | tf_op jit(solution)/shard_map/pack/pallas_call | solution.py:337
  30.8 3.9 %all-to-all-start = ((f32[32,8,256]{2,1,0:T(8,128)}), f32[32,8,256]{2,1,0:T(8,128)S(1)}, u32[]{:S(2)}, u32[]{:S(2)}) async-start(f32[32,8,256]{2,1,0:T(8,128)} %bitcast.27), calls=%async_computation | async-start | bytes 524288 | tf_op jit(solution)/shard_map/all_to_all | solution.py:346
  34.8 0.0 copy-start.4
  34.8 0.7 copy-done.4
  35.5 0.1 dynamic_slice.3
  35.6 9.7 %all-to-all-done.columns_ref = f32[32,8,256]{2,1,0:T(8,128)S(1)} async-done(((f32[32,8,256]{2,1,0:T(8,128)}), f32[32,8,256]{2,1,0:T(8,128)S(1)}, u32[]{:S(2)}, u32[]{:S(2)}) %all-to-all-start) | async-done | bytes 262176 | tf_op jit(solution)/shard_map/all_to_all | solution.py:346
  45.2 0.0 copy-start.2
  45.2 0.0 collective-permute-done.7.other_ref
  45.2 0.0 copy-start.1
  45.3 0.8 broadcast_in_dim.2.shift_ref
  46.0 0.0 copy-done
  46.0 0.0 copy-done.2
  46.0 0.3 copy-done.1
  46.3 27.0 %cg.1 = f32[32,2,8,256]{3,2,1,0:T(8,128)} custom-call(f32[32,8,256]{2,1,0:T(8,128)} %copy-done.2, f32[16,16,1024]{2,1,0:T(8,128)} %copy-done, f32[16,16,1024]{2,1,0:T(8,128)} %copy-done.1, f32[8,128]{1,0:T(8,128)} %broadcast_in_dim.2.shift_ref), custom_call_target="tpu_custom_call" | custom-call | tf_op jit(solution)/shard_map/cg/pallas_call | solution.py:356
  73.3 19.5 %all_to_all.10.back_ref = f32[32,2,8,256]{3,2,1,0:T(8,128)} all-to-all(f32[32,2,8,256]{3,2,1,0:T(8,128)} %cg.1), channel_id=1, replica_groups=mesh['gx'=4,'gy'=4,'gz'=2] {'gx','gy','gz'}, dimensions={0} | all-to-all | bytes 1048576 | tf_op jit(solution)/shard_map/all_to_all | solution.py:374
  92.9 2.0 %unpack.1 = (f32[4,4,4,4,256]{4,3,2,1,0:T(4,128)}, f32[4,4,4,4,256]{4,3,2,1,0:T(4,128)}) custom-call(f32[32,2,8,256]{3,2,1,0:T(8,128)} %all_to_all.10.back_ref), custom_call_target="tpu_custom_call" | custom-call | tf_op jit(solution)/shard_map/unpack/pallas_call | solution.py:377
  (6 shorter events, 0.2 us)
Async XLA Ops:
  2.8 7.9 %collective-permute-start.4 = (f32[16,1024]{1,0:T(8,128)}, f32[16,1024]{1,0:T(8,128)S(1)}, u32[]{:S(2)}, u32[]{:S(2)}) collective-permute-start(f32[16,1024]{1,0:T(8,128)} %block.1), channel_id=1, source_target_pairs={{0,6},{2,0},{4,2},{6,4},{1,7},{3,1},{5,3},{7,5},{8,14},{10,8},{12,... | collective-permute-start | bytes 196616 | tf_op jit(solution)/shard_map/ppermute | solution.py:27
  7.9 6.7 %collective-permute-start.3 = (f32[16,1024]{1,0:T(8,128)}, f32[16,1024]{1,0:T(8,128)S(1)}, u32[]{:S(2)}, u32[]{:S(2)}) collective-permute-start(f32[16,1024]{1,0:T(8,128)} %block.1), channel_id=1, source_target_pairs={{0,4},{2,6},{4,0},{6,2},{1,5},{3,7},{5,1},{7,3},{8,12},{10,14},{12... | collective-permute-start | bytes 196616 | tf_op jit(solution)/shard_map/ppermute | solution.py:27
  7.9 8.3 %collective-permute-start = (f32[16,1024]{1,0:T(8,128)}, f32[16,1024]{1,0:T(8,128)S(1)}, u32[]{:S(2)}, u32[]{:S(2)}) collective-permute-start(f32[16,1024]{1,0:T(8,128)} %block.1), channel_id=1, source_target_pairs={{0,2},{2,4},{4,6},{6,0},{1,3},{3,5},{5,7},{7,1},{8,10},{10,12},{12... | collective-permute-start | bytes 196616 | tf_op jit(solution)/shard_map/ppermute | solution.py:27
  14.6 1.6 %copy-start.3 = (f32[16,1024]{1,0:T(8,128)S(1)}, f32[16,1024]{1,0:T(8,128)}, u32[]{:S(2)}) copy-start(f32[16,1024]{1,0:T(8,128)} %block.1) | copy-start | bytes 196612
  14.6 5.3 %collective-permute-start.5 = (f32[2,16,1024]{2,1,0:T(8,128)S(1)}, f32[2,16,1024]{2,1,0:T(8,128)S(1)}, u32[]{:S(2)}, u32[]{:S(2)}) collective-permute-start(f32[2,16,1024]{2,1,0:T(8,128)S(1)} %get-tuple-element.9), channel_id=1, source_target_pairs={{0,1},{1,0},{2,3},{3,2},{4,5},{5,4},{6,7},{7,6},{8,9},{9,8},{10,11... | collective-permute-start | bytes 393224 | tf_op jit(solution)/shard_map/ppermute | solution.py:27
  16.2 5.3 %collective-permute-start.1 = (f32[2,16,1024]{2,1,0:T(8,128)S(1)}, f32[2,16,1024]{2,1,0:T(8,128)S(1)}, u32[]{:S(2)}, u32[]{:S(2)}) collective-permute-start(f32[2,16,1024]{2,1,0:T(8,128)S(1)} %get-tuple-element.7), channel_id=1, source_target_pairs={{0,16},{8,24},{16,0},{24,8},{1,17},{9,25},{17,1},{25,9},{2,18},{10... | collective-permute-start | bytes 393224 | tf_op jit(solution)/shard_map/ppermute | solution.py:32
  20.0 7.2 %collective-permute-start.6 = (f32[2,2,16,1024]{3,2,1,0:T(8,128)S(1)}, f32[2,2,16,1024]{3,2,1,0:T(8,128)S(1)}, u32[]{:S(2)}, u32[]{:S(2)}) collective-permute-start(f32[2,2,16,1024]{3,2,1,0:T(8,128)S(1)} %get-tuple-element.5), channel_id=1, source_target_pairs={{0,16},{8,24},{16,0},{24,8},{1,17},{9,25},{17,1},{25,9},{2,18},{10... | collective-permute-start | bytes 786440 | tf_op jit(solution)/shard_map/ppermute | solution.py:32
  21.6 7.0 %collective-permute-start.2 = (f32[2,2,16,1024]{3,2,1,0:T(8,128)S(1)}, f32[2,2,16,1024]{3,2,1,0:T(8,128)S(1)}, u32[]{:S(2)}, u32[]{:S(2)}) collective-permute-start(f32[2,2,16,1024]{3,2,1,0:T(8,128)S(1)} %get-tuple-element.3), channel_id=1, source_target_pairs={{0,1},{1,0},{2,3},{3,2},{4,5},{5,4},{6,7},{7,6},{8,9},{9,8},{10,11... | collective-permute-start | bytes 786440 | tf_op jit(solution)/shard_map/ppermute | solution.py:27
  28.7 17.3 %copy-start = (f32[16,16,1024]{2,1,0:T(8,128)}, f32[16,16,1024]{2,1,0:T(8,128)S(1)}, u32[]{:S(2)}) copy-start(f32[16,16,1024]{2,1,0:T(8,128)S(1)} %pad_maximum_fusion.own_ref) | copy-start | bytes 3145732
  28.7 16.5 %collective-permute-start.7 = (f32[16,16,1024]{2,1,0:T(8,128)S(1)}, f32[16,16,1024]{2,1,0:T(8,128)S(1)}, u32[]{:S(2)}, u32[]{:S(2)}) collective-permute-start(f32[16,16,1024]{2,1,0:T(8,128)S(1)} %pad_maximum_fusion.own_ref), channel_id=1, source_target_pairs={{0,8},{8,0},{16,24},{24,16},{1,9},{9,1},{17,25},{25,17},{2,10},{10... | collective-permute-start | bytes 3145736 | tf_op jit(solution)/shard_map/ppermute | solution.py:37
  30.8 14.4 %all-to-all-start = ((f32[32,8,256]{2,1,0:T(8,128)}), f32[32,8,256]{2,1,0:T(8,128)S(1)}, u32[]{:S(2)}, u32[]{:S(2)}) async-start(f32[32,8,256]{2,1,0:T(8,128)} %bitcast.27), calls=%async_computation | async-start | bytes 524288 | tf_op jit(solution)/shard_map/all_to_all | solution.py:346
  34.8 0.7 copy-start.4
  45.2 0.8 copy-start.2
  45.2 1.1 %copy-start.1 = (f32[16,16,1024]{2,1,0:T(8,128)}, f32[16,16,1024]{2,1,0:T(8,128)S(1)}, u32[]{:S(2)}) copy-start(f32[16,16,1024]{2,1,0:T(8,128)S(1)} %collective-permute-done.7.other_ref) | copy-start | bytes 3145732

commit v2 on v1

--- a/solution.py
+++ b/solution.py
@@ -2,14 +2,17 @@
 
 import jax
 import jax.numpy as jnp
+import numpy as np
 from jax import lax
 from jax.experimental import pallas as pl
 from jax.experimental.pallas import tpu as pltpu
 from jax.sharding import PartitionSpec as P
 
+
 ITERS = 3
 LANES = 128
 ROWS = 16
+PARTS = 8
 ALL = ("gx", "gy", "gz")
 
 half_offsets = [
@@ -50,67 +53,74 @@
     return own, core_swapped(own)
 
 
-def turn_groups(parts, group, seg):
-    count = len(parts)
-    bit = 1
-    while bit < count:
-        high = (group & bit) != 0
+def lane_plan(sizes, dx, dz):
+    count_x, _, count_z, lx, _, lz, _ = sizes
+    width = count_x * count_z * lx * lz
+    lane = np.arange(width)
+    tile, inner = lane // LANES, lane % LANES
+    part = (inner // (4 * lx * lz)) * 4 + (inner // (2 * lx * lz)) % 2 * 2 + (inner // lz) % 2
+    source = tile * PARTS + part
+    x = source // count_z * lx + (inner // (2 * lz)) % lx
+    z = source % count_z * lz + inner % lz
+    place = np.zeros((count_x * lx, count_z * lz), np.int64)
+    place[x, z] = lane
+    wanted = place[(x + dx) % (count_x * lx), (z + dz) % (count_z * lz)]
+    by = (lane - wanted) % width
+    return [(int(step), by == step) for step in sorted(set(by.tolist()), key=lambda n: -np.sum(by == n))]
+
+
+def all_plans(sizes):
+    return {name: lane_plan(sizes, *name) for name in ((0, 1), (0, -1), (1, 0), (-1, 0))}
+
+
+def turn_groups(parts, lane, strides):
+    bit = len(parts) // 2
+    for stride in strides:
+        high = (lane // stride) % 2 == 1
         turned = []
-        for index in range(count):
+        for index in range(len(parts)):
             other = parts[index ^ bit]
             if index & bit:
-                turned.append(jnp.where(high, parts[index], pltpu.roll(other, LANES - bit * seg, 1)))
+                turned.append(jnp.where(high, parts[index], pltpu.roll(other, LANES - stride, 1)))
             else:
-                turned.append(jnp.where(high, pltpu.roll(other, bit * seg, 1), parts[index]))
+                turned.append(jnp.where(high, pltpu.roll(other, stride, 1), parts[index]))
         parts = turned
-        bit *= 2
+        bit //= 2
     return parts
 
 
-def cg_kernel(sizes, columns_ref, own_ref, other_ref, shift_ref, out_ref, coef, field, image, answer, residual, ahead):
+def cg_kernel(sizes, columns_ref, own_ref, other_ref, shift_ref, mask_ref, out_ref, coef, field, image, answer, residual, ahead):
     count_x, count_y, count_z, lx, ly, lz, orbitals = sizes
-    seg = lx * lz
-    per = LANES // seg
-    width = count_x * count_z * seg
+    width = count_x * count_z * lx * lz
     high = count_y * ly
     chips = count_x // 2
     tiles = width // LANES
-    halves = ly * orbitals // per
-    group = lax.broadcasted_iota(jnp.int32, (1, LANES), 1) // seg
-    lane = lax.broadcasted_iota(jnp.int32, (1, width), 1)
-    at_z, at_x, at_gz = lane % lz, (lane // lz) % lx, (lane // seg) % count_z
-    step_x = seg * count_z - (lx - 1) * lz
-    step_z = seg - lz + 1
-    wrap_z = (count_z - 1) * seg + lz - 1
-
-    def roll(value, by):
-        return pltpu.roll(value, by % width, 1)
-
-    def from_next_z(value):
-        return jnp.where(at_z < lz - 1, roll(value, -1), jnp.where(at_gz < count_z - 1, roll(value, -step_z), roll(value, wrap_z)))
-
-    def from_last_z(value):
-        return jnp.where(at_z > 0, roll(value, 1), jnp.where(at_gz > 0, roll(value, step_z), roll(value, -wrap_z)))
-
-    def from_next_x(value):
-        return jnp.where(at_x < lx - 1, roll(value, -lz), roll(value, -step_x))
-
-    def from_last_x(value):
-        return jnp.where(at_x > 0, roll(value, lz), roll(value, step_x))
+    lane = lax.broadcasted_iota(jnp.int32, (1, LANES), 1)
+    strides = (4 * lx * lz, 2 * lx * lz, lz)
+    moves, row = {}, 0
+    for name, plan in all_plans(sizes).items():
+        moves[name] = [(plan[0][0], None)]
+        for by, _ in plan[1:]:
+            moves[name].append((by, mask_ref[row : row + 1, :] != 0))
+            row += 1
+
+    def take(value, name):
+        result = None
+        for by, mask in moves[name]:
+            rolled = pltpu.roll(value, by, 1)
+            result = rolled if mask is None else jnp.where(mask, rolled, result)
+        return result
 
     def device_of(source, gy):
         return ((source // count_z) * count_y + gy) * count_z + source % count_z
 
     for gy in range(count_y):
         for tile in range(tiles):
-            for half in range(halves):
-                parts = [
-                    columns_ref[device_of(tile * per + p, gy), :, half * LANES : (half + 1) * LANES]
-                    for p in range(per)
-                ]
-                for g, value in enumerate(turn_groups(parts, group, seg)):
-                    y, orb = divmod(half * per + g, orbitals)
-                    field[gy * ly + y, orb, :, tile * LANES : (tile + 1) * LANES] = value
+            for half in range(ly // 2):
+                lanes = slice(half * LANES, (half + 1) * LANES)
+                parts = [columns_ref[device_of(tile * PARTS + p, gy), :, lanes] for p in range(PARTS)]
+                for g, value in enumerate(turn_groups(parts, lane, strides)):
+                    field[gy * ly + half * 2 + g % 2, g // 2, :, tile * LANES : (tile + 1) * LANES] = value
 
     my_x, my_y, my_z = lax.axis_index("gx"), lax.axis_index("gy"), lax.axis_index("gz")
     my_chip, my_core = my_x // 2, my_x % 2
@@ -121,8 +131,8 @@
         near = away < half_y
         for tile in range(tiles):
             slots, cores = [], []
-            for p in range(per):
-                gx, gz = divmod(tile * per + p, count_z)
+            for p in range(PARTS):
+                gx, gz = divmod(tile * PARTS + p, count_z)
                 across = lax.rem(my_chip - gx // 2 + chips, chips)
                 up = lax.rem(my_z - gz + count_z, count_z)
                 slots.append(
@@ -133,15 +143,14 @@
                     )
                 )
                 cores.append(gx % 2 == my_core)
-            for part in range(orbitals * orbitals * ly // per):
+            for part in range(orbitals * orbitals // 2):
                 lanes = slice(part * LANES, (part + 1) * LANES)
                 parts = [
                     jnp.where(core, own_ref[slot, :, lanes], other_ref[slot, :, lanes])
                     for slot, core in zip(slots, cores)
                 ]
-                for g, value in enumerate(turn_groups(parts, group, seg)):
-                    pair, y = divmod(part * per + g, ly)
-                    coef[gy * ly + y, pair, :, tile * LANES : (tile + 1) * LANES] = value
+                for g, value in enumerate(turn_groups(parts, lane, strides)):
+                    coef[gy * ly + g % ly, part * 2 + g // ly, :, tile * LANES : (tile + 1) * LANES] = value
         return carry
 
     lax.fori_loop(0, count_y, fill, 0)
@@ -160,19 +169,23 @@
 
     directions = ((0, 1), (0, -1), (1, 0), (1, 1), (1, -1))
 
-    def spread(y, carry):
+    def spread(y):
+        rows = []
         for orb in range(orbitals):
             value = field[y, orb]
-            above, below = from_next_z(value), from_last_z(value)
-            ahead[0, y, orb] = above
-            ahead[1, y, orb] = below
-            ahead[2, y, orb] = from_next_x(value)
-            ahead[3, y, orb] = from_next_x(above)
-            ahead[4, y, orb] = from_next_x(below)
-        return carry
+            above, below = take(value, (0, 1)), take(value, (0, -1))
+            rows.append((above, below, take(value, (1, 0)), take(above, (1, 0)), take(below, (1, 0))))
+        return rows
+
+    def keep(y, rows):
+        for orb, values in enumerate(rows):
+            for which, value in enumerate(values):
+                ahead[which, y, orb] = value
 
     def apply(y, total):
         rows = {0: y, 1: lax.rem(y + 1, high), -1: lax.rem(y + high - 1, high)}
+        coming = lax.rem(y + 2, high)
+        spread_rows = spread(coming)
 
         def factor(row, i, j, k):
             return coef[row, i * orbitals + j, k : k + 1, :]
@@ -203,18 +216,20 @@
                         term = factor(row, j, i, k) * value
                         sums[i] = term if sums[i] is None else sums[i] + term
             if third == 1:
-                sums = [from_last_z(value) for value in sums]
+                sums = [take(value, (0, -1)) for value in sums]
             elif third == -1:
-                sums = [from_next_z(value) for value in sums]
+                sums = [take(value, (0, 1)) for value in sums]
             landing[first] = [a + b for a, b in zip(landing[first], sums)] if first in landing else sums
         for i in range(orbitals):
-            value = result[i] + landing[0][i] + from_last_x(landing[1][i])
+            value = result[i] + landing[0][i] + take(landing[1][i], (-1, 0))
             image[y, i] = value
             total = total + value * here[i]
+        keep(coming, spread_rows)
         return total
 
     for iteration in range(ITERS):
-        lax.fori_loop(0, high, spread, 0)
+        for y in (high - 1, 0, 1):
+            keep(y, spread(y))
         product = jnp.sum(lax.fori_loop(0, high, apply, zero), axis=1, keepdims=True)
         alpha = norm_now / product
 
@@ -243,13 +258,11 @@
     for which, source in enumerate((answer, residual)):
         for gy in range(count_y):
             for tile in range(tiles):
-                for half in range(halves):
-                    parts = []
-                    for g in range(per):
-                        y, orb = divmod(half * per + g, orbitals)
-                        parts.append(source[gy * ly + y, orb, :, tile * LANES : (tile + 1) * LANES])
-                    for p, value in enumerate(turn_groups(parts, group, seg)):
-                        out_ref[device_of(tile * per + p, gy), which, :, half * LANES : (half + 1) * LANES] = value
+                for half in range(ly // 2):
+                    lanes = slice(tile * LANES, (tile + 1) * LANES)
+                    parts = [source[gy * ly + half * 2 + g % 2, g // 2, :, lanes] for g in range(PARTS)]
+                    for p, value in enumerate(turn_groups(parts, lane, strides)):
+                        out_ref[device_of(tile * PARTS + p, gy), which, :, half * LANES : (half + 1) * LANES] = value
 
 
 def block_kernel(bonds_ref, open_ref, onsite_ref, levels_ref, out_ref, rows):
@@ -266,7 +279,7 @@
                 if i == j:
                     local = local + levels_ref[i, x]
                 for y in range(ly):
-                    row = (((i * orbitals + j) * ly + y) * lx + x) * lz
+                    row = ((((i * orbitals + j) * (ly // 2) + y // 2) * lx + x) * 2 + y % 2) * lz
                     mask = open_ref[x * ly + y].astype(jnp.float32)
                     rows[row : row + lz, :bonds] = bonds_ref[((i * orbitals + j) * lx + x) * ly + y] * mask
                     rows[row : row + lz, bonds : bonds + lz] = eye * local[y : y + 1, :]
@@ -281,10 +294,10 @@
     for x in range(lx):
         for y in range(ly):
             for z in range(lz):
-                base = y * orbitals * lx * lz + x * lz + z
+                base = ((y // 2 * orbitals * lx + x) * 2 + y % 2) * lz + z
                 for tile in range(rows.shape[0]):
                     lanes = slice(tile * LANES, (tile + 1) * LANES)
-                    rows[tile, pl.ds(base, orbitals, stride=lx * lz), :] = field_ref[x, y, z, :, lanes]
+                    rows[tile, pl.ds(base, orbitals, stride=2 * lx * lz), :] = field_ref[x, y, z, :, lanes]
     for tile in range(rows.shape[0]):
         out_ref[tile * LANES : (tile + 1) * LANES, :] = jnp.transpose(rows[tile])
 
@@ -298,10 +311,10 @@
         for x in range(lx):
             for y in range(ly):
                 for z in range(lz):
-                    base = y * orbitals * lx * lz + x * lz + z
+                    base = ((y // 2 * orbitals * lx + x) * 2 + y % 2) * lz + z
                     for tile in range(rows.shape[1]):
                         lanes = slice(tile * LANES, (tile + 1) * LANES)
-                        out_ref[x, y, z, :, lanes] = rows[which, tile, pl.ds(base, orbitals, stride=lx * lz), :]
+                        out_ref[x, y, z, :, lanes] = rows[which, tile, pl.ds(base, orbitals, stride=2 * lx * lz), :]
 
 
 def per_device(right_side, bond_blocks, bond_open, onsite_blocks, orbital_levels, column_shift):
@@ -310,11 +323,10 @@
     devices = count_x * count_y * count_z
     own_columns = columns // devices
     padded = -(-own_columns // 8) * 8
-    seg = lx * lz
-    width = count_x * count_z * seg
+    width = count_x * count_z * lx * lz
     high = count_y * ly
-    assert LANES % seg == 0 and width % LANES == 0 and count_x % 2 == 0 and count_y % 2 == 0
-    assert (ly * orbitals) % (LANES // seg) == 0 and columns % devices == 0
+    assert (lx, ly, lz, orbitals) == (4, 4, 4, 4) and columns % devices == 0
+    assert count_x % 2 == 0 and count_y % 2 == 0 and count_x * count_z % PARTS == 0
 
     atoms = lx * ly * lz
     bonds = bond_blocks.shape[0]
@@ -352,12 +364,14 @@
     shift = jnp.broadcast_to(shift[:, None], (padded, width))
 
     sizes = (count_x, count_y, count_z, lx, ly, lz, orbitals)
+    masks = [lanes for plan in all_plans(sizes).values() for _, lanes in plan[1:]]
+    masks = jnp.asarray(np.stack(masks).astype(np.int32))
     state = pltpu.VMEM((high, orbitals, padded, width), jnp.float32)
     out = pl.pallas_call(
         functools.partial(cg_kernel, sizes),
-        out_shape=jax.ShapeDtypeStruct((devices, 2, padded, ly * orbitals * seg), jnp.float32),
-        in_specs=[pl.BlockSpec(memory_space=pltpu.VMEM)] * 4,
-        out_specs=pl.BlockSpec(memory_space=pltpu.VMEM),
+        out_shape=jax.ShapeDtypeStruct((devices, 2, padded, orbitals * lx * ly * lz), jnp.float32),
+        in_specs=[vmem] * 5,
+        out_specs=vmem,
         scratch_shapes=[
             pltpu.VMEM((high, orbitals * orbitals, ROWS, width), jnp.float32),
             state,
@@ -366,9 +380,9 @@
             state,
             pltpu.VMEM((5, high, orbitals, padded, width), jnp.float32),
         ],
-        compiler_params=pltpu.CompilerParams(vmem_limit_bytes=56 * 1024 * 1024),
+        compiler_params=pltpu.CompilerParams(vmem_limit_bytes=(8 + 24 * width // 512) * 1024 * 1024 * 2),
         name="cg",
-    )(received, own, other, shift)
+    )(received, own, other, shift, masks)
     if padded != own_columns:
         out = out[:, :, :own_columns]
     back = lax.all_to_all(out, ALL, 0, 0, tiled=True)

time: 95.3 us -> 83.7 us (0.88)
  Pallas kernels: 33.3 us -> 23.5 us
  local copies, waits for them, and re-layouts: 1.84 us -> 0.82 us
    pallas_call x1, Pallas kernels: 27 us -> 17.2 us  [per_device(): pl.pallas_call(functools.partial(cg_kernel, sizes), out_shape=jax.ShapeDt...]
where the time goes in v2:
time: 83.7 us; the launch traced here: 83.4 us
  Pallas kernels  23.5 us (28%)
  waiting for transfers between devices  22.8 us (27%)
  blocking collectives  18.7 us (22%)
  starting transfers between devices  16.5 us (20%)
    all_to_all x1, blocking collectives, per_device(): back = lax.all_to_all(out, ALL, 0, 0, tiled=True)  18.7 us
    pallas_call x1, Pallas kernels, per_device(): pl.pallas_call(functools.partial(cg_kernel, sizes), out_shape=jax.ShapeDt...  17.2 us
    all_to_all x1, waiting for transfers between devices, per_device(): received = lax.all_to_all(packed, ALL, 0, 0, tiled=True)  9.67 us
    ppermute x5, starting transfers between devices, shifted(): lax.ppermute(value, axis, [(i, (i + by) % peers) for i in range(peers)])  9.26 us
    ppermute x5, waiting for transfers between devices, shifted(): lax.ppermute(value, axis, [(i, (i + by) % peers) for i in range(peers)])  9.08 us
    ppermute x2, waiting for transfers between devices, chip_shifted(): lax.ppermute(value, 'gx', [(i, (i + 2 * by) % peers) for i in range(peers)])  4.05 us
    all_to_all x1, starting transfers between devices, per_device(): received = lax.all_to_all(packed, ALL, 0, 0, tiled=True)  4.04 us
    ppermute x2, starting transfers between devices, chip_shifted(): lax.ppermute(value, 'gx', [(i, (i + 2 * by) % peers) for i in range(peers)])  3.11 us
  transfers between devices with their start and end apart: 9, of which 6 were waited for; matrix products, arithmetic and copies ran while one was open for 0% of the time, Pallas kernels for 2%

profile of v2, /device:TPU:0, one launch (start us, length us, event | category | flops | bytes accessed | tf_op | source)
XLA Modules:
  0.0 83.4 jit_solution(5454826862595544232)
XLA Ops:
  0.6 2.2 %block.1 = f32[16,1024]{1,0:T(8,128)} custom-call(f32[256,4,13]{2,1,0:T(4,128)} %bitcast.28, s32[16,4,13]{2,1,0:T(4,128)} %bitcast.37, f32[4,4,4,4,4]{4,3,2,1,0:T(4,128)} %onsite_ref.1, f32[4,4,4,4]{3,2,1,0:T(4,128)} %levels_ref.1), custom_call_target="tpu_custom_call" | custom-call | tf_op jit(solution)/shard_map/block/pallas_call | solution.py:334
  2.8 5.1 %collective-permute-start.4 = (f32[16,1024]{1,0:T(8,128)}, f32[16,1024]{1,0:T(8,128)S(1)}, u32[]{:S(2)}, u32[]{:S(2)}) collective-permute-start(f32[16,1024]{1,0:T(8,128)} %block.1), channel_id=1, source_target_pairs={{0,6},{2,0},{4,2},{6,4},{1,7},{3,1},{5,3},{7,5},{8,14},{10,8},{12,... | collective-permute-start | bytes 196616 | tf_op jit(solution)/shard_map/ppermute | solution.py:30
  7.9 0.0 collective-permute-start.3
  7.9 1.0 %collective-permute-start = (f32[16,1024]{1,0:T(8,128)}, f32[16,1024]{1,0:T(8,128)S(1)}, u32[]{:S(2)}, u32[]{:S(2)}) collective-permute-start(f32[16,1024]{1,0:T(8,128)} %block.1), channel_id=1, source_target_pairs={{0,2},{2,4},{4,6},{6,0},{1,3},{3,5},{5,7},{7,1},{8,10},{10,12},{12... | collective-permute-start | bytes 196616 | tf_op jit(solution)/shard_map/ppermute | solution.py:30
  8.9 1.8 %collective-permute-done.4 = f32[16,1024]{1,0:T(8,128)S(1)} collective-permute-done((f32[16,1024]{1,0:T(8,128)}, f32[16,1024]{1,0:T(8,128)S(1)}, u32[]{:S(2)}, u32[]{:S(2)}) %collective-permute-start.4) | collective-permute-done | bytes 65568 | tf_op jit(solution)/shard_map/ppermute | solution.py:30
  10.7 3.9 %collective-permute-done.3 = f32[16,1024]{1,0:T(8,128)S(1)} collective-permute-done((f32[16,1024]{1,0:T(8,128)}, f32[16,1024]{1,0:T(8,128)S(1)}, u32[]{:S(2)}, u32[]{:S(2)}) %collective-permute-start.3) | collective-permute-done | bytes 65568 | tf_op jit(solution)/shard_map/ppermute | solution.py:30
  14.6 0.0 copy-start.1
  14.6 1.6 %collective-permute-start.5 = (f32[2,16,1024]{2,1,0:T(8,128)S(1)}, f32[2,16,1024]{2,1,0:T(8,128)S(1)}, u32[]{:S(2)}, u32[]{:S(2)}) collective-permute-start(f32[2,16,1024]{2,1,0:T(8,128)S(1)} %get-tuple-element.9), channel_id=1, source_target_pairs={{0,1},{1,0},{2,3},{3,2},{4,5},{5,4},{6,7},{7,6},{8,9},{9,8},{10,11... | collective-permute-start | bytes 393224 | tf_op jit(solution)/shard_map/ppermute | solution.py:30
  16.2 0.0 collective-permute-done
  16.2 0.0 copy-done.1
  16.2 1.6 %collective-permute-start.1 = (f32[2,16,1024]{2,1,0:T(8,128)S(1)}, f32[2,16,1024]{2,1,0:T(8,128)S(1)}, u32[]{:S(2)}, u32[]{:S(2)}) collective-permute-start(f32[2,16,1024]{2,1,0:T(8,128)S(1)} %get-tuple-element.7), channel_id=1, source_target_pairs={{0,16},{8,24},{16,0},{24,8},{1,17},{9,25},{17,1},{25,9},{2,18},{10... | collective-permute-start | bytes 393224 | tf_op jit(solution)/shard_map/ppermute | solution.py:35
  17.8 2.1 %collective-permute-done.5 = f32[2,16,1024]{2,1,0:T(8,128)S(1)} collective-permute-done((f32[2,16,1024]{2,1,0:T(8,128)S(1)}, f32[2,16,1024]{2,1,0:T(8,128)S(1)}, u32[]{:S(2)}, u32[]{:S(2)}) %collective-permute-start.5) | collective-permute-done | bytes 131104 | tf_op jit(solution)/shard_map/ppermute | solution.py:30
  20.0 1.6 %collective-permute-start.6 = (f32[2,2,16,1024]{3,2,1,0:T(8,128)S(1)}, f32[2,2,16,1024]{3,2,1,0:T(8,128)S(1)}, u32[]{:S(2)}, u32[]{:S(2)}) collective-permute-start(f32[2,2,16,1024]{3,2,1,0:T(8,128)S(1)} %get-tuple-element.5), channel_id=1, source_target_pairs={{0,16},{8,24},{16,0},{24,8},{1,17},{9,25},{17,1},{25,9},{2,18},{10... | collective-permute-start | bytes 786440 | tf_op jit(solution)/shard_map/ppermute | solution.py:35
  21.5 0.0 collective-permute-done.1
  21.6 1.6 %collective-permute-start.2 = (f32[2,2,16,1024]{3,2,1,0:T(8,128)S(1)}, f32[2,2,16,1024]{3,2,1,0:T(8,128)S(1)}, u32[]{:S(2)}, u32[]{:S(2)}) collective-permute-start(f32[2,2,16,1024]{3,2,1,0:T(8,128)S(1)} %get-tuple-element.3), channel_id=1, source_target_pairs={{0,1},{1,0},{2,3},{3,2},{4,5},{5,4},{6,7},{7,6},{8,9},{9,8},{10,11... | collective-permute-start | bytes 786440 | tf_op jit(solution)/shard_map/ppermute | solution.py:30
  23.2 4.0 %collective-permute-done.6 = f32[2,2,16,1024]{3,2,1,0:T(8,128)S(1)} collective-permute-done((f32[2,2,16,1024]{3,2,1,0:T(8,128)S(1)}, f32[2,2,16,1024]{3,2,1,0:T(8,128)S(1)}, u32[]{:S(2)}, u32[]{:S(2)}) %collective-permute-start.6) | collective-permute-done | bytes 262176 | tf_op jit(solution)/shard_map/ppermute | solution.py:35
  27.3 1.3 %collective-permute-done.2 = f32[2,2,16,1024]{3,2,1,0:T(8,128)S(1)} collective-permute-done((f32[2,2,16,1024]{3,2,1,0:T(8,128)S(1)}, f32[2,2,16,1024]{3,2,1,0:T(8,128)S(1)}, u32[]{:S(2)}, u32[]{:S(2)}) %collective-permute-start.2) | collective-permute-done | bytes 262176 | tf_op jit(solution)/shard_map/ppermute | solution.py:30
  28.6 0.1 pad_maximum_fusion.own_ref
  28.7 0.1 collective-permute-start.7
  28.8 1.9 %pack.1 = f32[256,256]{1,0:T(8,128)} custom-call(f32[4,4,4,4,256]{4,3,2,1,0:T(4,128)} %field_ref.1), custom_call_target="tpu_custom_call" | custom-call | tf_op jit(solution)/shard_map/pack/pallas_call | solution.py:349
  30.7 4.0 %all-to-all-start = ((f32[32,8,256]{2,1,0:T(8,128)}), f32[32,8,256]{2,1,0:T(8,128)S(1)}, u32[]{:S(2)}, u32[]{:S(2)}) async-start(f32[32,8,256]{2,1,0:T(8,128)} %bitcast.27), calls=%async_computation | async-start | bytes 524288 | tf_op jit(solution)/shard_map/all_to_all | solution.py:358
  34.8 0.0 copy-start.2
  34.8 0.7 copy-done.2
  35.5 0.1 dynamic_slice.3
  35.5 0.0 copy-start
  35.5 9.7 %all-to-all-done.columns_ref = f32[32,8,256]{2,1,0:T(8,128)S(1)} async-done(((f32[32,8,256]{2,1,0:T(8,128)}), f32[32,8,256]{2,1,0:T(8,128)S(1)}, u32[]{:S(2)}, u32[]{:S(2)}) %all-to-all-start) | async-done | bytes 262176 | tf_op jit(solution)/shard_map/all_to_all | solution.py:358
  45.2 0.0 collective-permute-done.7.other_ref
  45.2 0.1 broadcast_in_dim.2.shift_ref
  45.3 0.0 copy-done
  45.3 17.2 %cg.1 = f32[32,2,8,256]{3,2,1,0:T(8,128)S(1)} custom-call(f32[32,8,256]{2,1,0:T(8,128)S(1)} %all-to-all-done.columns_ref, f32[16,16,1024]{2,1,0:T(8,128)S(1)} %pad_maximum_fusion.own_ref, f32[16,16,1024]{2,1,0:T(8,128)S(1)} %collective-permute-done.7.other_ref, f32[8,128]{1,0:T(8,128)S(1)} %broadcast_in_dim.2.shift_ref, s32[2,128]{1,0:T(2,128)S(1)} %copy-done), custom_call_target="tpu_custom_call" | custom-call | tf_op jit(solution)/shard_map/cg/pallas_call | solution.py:370
  62.5 18.7 %all_to_all.10.back_ref = f32[32,2,8,256]{3,2,1,0:T(8,128)} all-to-all(f32[32,2,8,256]{3,2,1,0:T(8,128)S(1)} %cg.1), channel_id=1, replica_groups=mesh['gx'=4,'gy'=4,'gz'=2] {'gx','gy','gz'}, dimensions={0} | all-to-all | bytes 1048576 | tf_op jit(solution)/shard_map/all_to_all | solution.py:388
  81.1 2.2 %unpack.1 = (f32[4,4,4,4,256]{4,3,2,1,0:T(4,128)}, f32[4,4,4,4,256]{4,3,2,1,0:T(4,128)}) custom-call(f32[32,2,8,256]{3,2,1,0:T(8,128)} %all_to_all.10.back_ref), custom_call_target="tpu_custom_call" | custom-call | tf_op jit(solution)/shard_map/unpack/pallas_call | solution.py:391
  (6 shorter events, 0.2 us)
Async XLA Ops:
  2.8 7.9 %collective-permute-start.4 = (f32[16,1024]{1,0:T(8,128)}, f32[16,1024]{1,0:T(8,128)S(1)}, u32[]{:S(2)}, u32[]{:S(2)}) collective-permute-start(f32[16,1024]{1,0:T(8,128)} %block.1), channel_id=1, source_target_pairs={{0,6},{2,0},{4,2},{6,4},{1,7},{3,1},{5,3},{7,5},{8,14},{10,8},{12,... | collective-permute-start | bytes 196616 | tf_op jit(solution)/shard_map/ppermute | solution.py:30
  7.9 6.7 %collective-permute-start.3 = (f32[16,1024]{1,0:T(8,128)}, f32[16,1024]{1,0:T(8,128)S(1)}, u32[]{:S(2)}, u32[]{:S(2)}) collective-permute-start(f32[16,1024]{1,0:T(8,128)} %block.1), channel_id=1, source_target_pairs={{0,4},{2,6},{4,0},{6,2},{1,5},{3,7},{5,1},{7,3},{8,12},{10,14},{12... | collective-permute-start | bytes 196616 | tf_op jit(solution)/shard_map/ppermute | solution.py:30
  7.9 8.3 %collective-permute-start = (f32[16,1024]{1,0:T(8,128)}, f32[16,1024]{1,0:T(8,128)S(1)}, u32[]{:S(2)}, u32[]{:S(2)}) collective-permute-start(f32[16,1024]{1,0:T(8,128)} %block.1), channel_id=1, source_target_pairs={{0,2},{2,4},{4,6},{6,0},{1,3},{3,5},{5,7},{7,1},{8,10},{10,12},{12... | collective-permute-start | bytes 196616 | tf_op jit(solution)/shard_map/ppermute | solution.py:30
  14.6 1.6 %copy-start.1 = (f32[16,1024]{1,0:T(8,128)S(1)}, f32[16,1024]{1,0:T(8,128)}, u32[]{:S(2)}) copy-start(f32[16,1024]{1,0:T(8,128)} %block.1) | copy-start | bytes 196612
  14.6 5.3 %collective-permute-start.5 = (f32[2,16,1024]{2,1,0:T(8,128)S(1)}, f32[2,16,1024]{2,1,0:T(8,128)S(1)}, u32[]{:S(2)}, u32[]{:S(2)}) collective-permute-start(f32[2,16,1024]{2,1,0:T(8,128)S(1)} %get-tuple-element.9), channel_id=1, source_target_pairs={{0,1},{1,0},{2,3},{3,2},{4,5},{5,4},{6,7},{7,6},{8,9},{9,8},{10,11... | collective-permute-start | bytes 393224 | tf_op jit(solution)/shard_map/ppermute | solution.py:30
  16.2 5.3 %collective-permute-start.1 = (f32[2,16,1024]{2,1,0:T(8,128)S(1)}, f32[2,16,1024]{2,1,0:T(8,128)S(1)}, u32[]{:S(2)}, u32[]{:S(2)}) collective-permute-start(f32[2,16,1024]{2,1,0:T(8,128)S(1)} %get-tuple-element.7), channel_id=1, source_target_pairs={{0,16},{8,24},{16,0},{24,8},{1,17},{9,25},{17,1},{25,9},{2,18},{10... | collective-permute-start | bytes 393224 | tf_op jit(solution)/shard_map/ppermute | solution.py:35
  20.0 7.2 %collective-permute-start.6 = (f32[2,2,16,1024]{3,2,1,0:T(8,128)S(1)}, f32[2,2,16,1024]{3,2,1,0:T(8,128)S(1)}, u32[]{:S(2)}, u32[]{:S(2)}) collective-permute-start(f32[2,2,16,1024]{3,2,1,0:T(8,128)S(1)} %get-tuple-element.5), channel_id=1, source_target_pairs={{0,16},{8,24},{16,0},{24,8},{1,17},{9,25},{17,1},{25,9},{2,18},{10... | collective-permute-start | bytes 786440 | tf_op jit(solution)/shard_map/ppermute | solution.py:35
  21.6 7.0 %collective-permute-start.2 = (f32[2,2,16,1024]{3,2,1,0:T(8,128)S(1)}, f32[2,2,16,1024]{3,2,1,0:T(8,128)S(1)}, u32[]{:S(2)}, u32[]{:S(2)}) collective-permute-start(f32[2,2,16,1024]{3,2,1,0:T(8,128)S(1)} %get-tuple-element.3), channel_id=1, source_target_pairs={{0,1},{1,0},{2,3},{3,2},{4,5},{5,4},{6,7},{7,6},{8,9},{9,8},{10,11... | collective-permute-start | bytes 786440 | tf_op jit(solution)/shard_map/ppermute | solution.py:30
  28.7 16.5 %collective-permute-start.7 = (f32[16,16,1024]{2,1,0:T(8,128)S(1)}, f32[16,16,1024]{2,1,0:T(8,128)S(1)}, u32[]{:S(2)}, u32[]{:S(2)}) collective-permute-start(f32[16,16,1024]{2,1,0:T(8,128)S(1)} %pad_maximum_fusion.own_ref), channel_id=1, source_target_pairs={{0,8},{8,0},{16,24},{24,16},{1,9},{9,1},{17,25},{25,17},{2,10},{10... | collective-permute-start | bytes 3145736 | tf_op jit(solution)/shard_map/ppermute | solution.py:40
  30.7 14.5 %all-to-all-start = ((f32[32,8,256]{2,1,0:T(8,128)}), f32[32,8,256]{2,1,0:T(8,128)S(1)}, u32[]{:S(2)}, u32[]{:S(2)}) async-start(f32[32,8,256]{2,1,0:T(8,128)} %bitcast.27), calls=%async_computation | async-start | bytes 524288 | tf_op jit(solution)/shard_map/all_to_all | solution.py:358
  34.8 0.7 copy-start.2
  35.5 9.8 %copy-start = (s32[2,128]{1,0:T(2,128)S(1)}, s32[2,128]{1,0:T(2,128)}, u32[]{:S(2)}) copy-start(s32[2,128]{1,0:T(2,128)} %constant.23.clone.mask_ref) | copy-start | bytes 3076
